TPU v7x, 256 devices: a whole 4x4x8 slice. The times are simulated.
256 devices in a mesh: rep: 4 (over z_hi), px: 8 (over x, core), py: 8 (over z_lo, y).
Axes of the slice: x: 4, y: 4, z: 8 (z_hi: 4, z_lo: 2; z = z_hi * 2 + z_lo), core: 2. Of those that a mesh axis runs over, the one named last changes fastest.
Arguments:
- state: float32 [12, 2, 192, 96, 256], P('rep', None, 'px', 'py'), parts along dimension 0, may hold values from -6 to 6
- cotangent: float32 [12, 2, 192, 96, 256], P('rep', None, 'px', 'py'), parts along dimension 0, may hold values from -6 to 6
- w_in: bfloat16 [512, 192], replicated, may hold values from -0.4375 to 0.4375
- b_in: float32 [512], replicated, may hold values from -5 to 5
- w_out: bfloat16 [192, 512], replicated, may hold values from -0.25 to 0.25
Outputs:
- state_grad: float32 [12, 2, 192, 96, 256], P('rep', None, 'px', 'py'), parts along dimension 0
- grad_in: float32 [512, 768], P(('px', 'py'), 'rep'), parts along dimension 1
- grad_out: float32 [768, 512], P('rep', ('px', 'py')), parts along dimension 0
- grad_bias: float32 [4, 512], P('rep', ('px', 'py')), parts along dimension 0
There are 4 independent parts, one for each index of `rep`. A program takes and returns all parts, laid end to end along the dimension named above; an argument that names none is the same for every part. Nothing has to cross between parts.
All inputs are finite; a program needn't handle non-finite values.
Results may differ from a plain program's by a relative error of at most 0.0065.
The roundings to bfloat16 on the way count: a program that leaves them out, or rounds other values in their place, can miss the bound.
Values may be sent and summed in bfloat16 or wider, within the bound.
A program may use at most 128 MiB of HBM per device.

v0:
```python
import numpy as np

import jax
import jax.numpy as jnp
from jax import lax
from jax.experimental import pallas as pl
from jax.experimental.pallas import tpu as pltpu
from jax.sharding import PartitionSpec as P

F32 = jnp.float32
BF16 = jnp.bfloat16
MESH = pl.DeviceIdType.MESH
NN = (((1,), (0,)), ((), ()))
NT = (((1,), (1,)), ((), ()))
TN = (((0,), (0,)), ((), ()))

NG, KY, KZ, HID, FEAT = 256, 192, 96, 512, 192
CUT = NG // 3
NU_DT = 5e-05
TIME_STEP = 0.01
FORCING = 20.0
NDEV = 64
WY, WZ = 24, 12
SLOT = 48
INV = 8
INV_W = INV * 3 * SLOT
FWD_W = 16 * SLOT
SEND_W = FWD_W + 256
PITCH = 72


def dot(a, b, dims=NN, **kw):
    return lax.dot_general(a, b, dims, preferred_element_type=F32, **kw)


def make_tables():
    bf = jnp.bfloat16

    def angle(k, x):
        theta = 2 * np.pi * ((np.asarray(k)[:, None] % NG) * np.asarray(x)[None, :] % NG) / NG
        return np.cos(theta) / np.sqrt(NG), np.sin(theta) / np.sqrt(NG)

    order_x = np.arange(NG).reshape(64, 4).T.reshape(-1)
    c, s = angle(order_x, np.arange(NG))
    tx = np.concatenate([c, -s], axis=1)
    order = np.arange(NG).reshape(64, 4).T.reshape(-1)
    ids = np.arange(KY)
    ky = np.where(ids < KY // 2, ids, ids - KY)
    c, s = angle(ky, order)
    top = np.concatenate([c, s], axis=1).reshape(8, 1, WY, 2 * NG)
    low = np.concatenate([-s, c], axis=1).reshape(8, 1, WY, 2 * NG)
    kcol = ky.reshape(8, 1, WY, 1)
    ty = np.concatenate([top, low], axis=1).reshape(2 * KY, 2 * NG)
    tyk = np.concatenate([-kcol * low, kcol * top], axis=1).reshape(2 * KY, 2 * NG)
    kz = (np.arange(8)[None, :, None] * WZ + np.arange(3)[:, None, None] * 4 + np.arange(4)[None, None, :]).reshape(-1)
    c, s = angle(order, kz)
    tz = np.concatenate([c, -s], axis=1)
    kk = np.concatenate([kz, kz])[None, :]
    tzk = np.concatenate([s, c], axis=1) * kk
    perm = np.zeros((FEAT, FEAT), np.float32)
    src = np.arange(FEAT).reshape(3, 4, 4, 4).transpose(2, 0, 1, 3).reshape(-1)
    perm[src, np.arange(FEAT)] = 1.0
    back = np.zeros((256, 256), np.float32)
    back[:FEAT, :FEAT] = perm.T
    back[FEAT, FEAT] = 1.0
    two = lambda t: np.concatenate([t, t], axis=0)
    arrays = dict(tx=tx, ty=two(ty), tyk=two(tyk), tz=tz, tzk=tzk, tzt=tz.T, tzkt=tzk.T, perm=perm)
    out = {k: np.asarray(v, np.float32).astype(bf) for k, v in arrays.items()}
    out["back"] = back
    return out


def waves_of(m, j, l):
    kz_id = l * WZ + m
    kz = kz_id.astype(F32)
    a = lax.broadcasted_iota(jnp.int32, (WY, NG), 0) + j * WY
    n = lax.broadcasted_iota(jnp.int32, (WY, NG), 1)
    ky = jnp.where(a < KY // 2, a, a - KY).astype(F32)
    kx = jnp.where(n < NG // 2, n, n - NG).astype(F32)
    keep = (jnp.abs(kx) <= CUT) & (jnp.abs(ky) <= CUT) & (kz <= float(CUT))
    retained = keep.astype(F32)
    square = kx * kx + ky * ky + kz * kz
    damping = jnp.exp(-NU_DT * square)
    weight = jnp.where(kz_id == 0, 1.0, 2.0).astype(F32)
    return kx, ky, kz, retained, square, damping, weight


def spectral_out(state_ref, cot_ref, tx_ref, a_ref, s_ref, a32):
    j, l = lax.axis_index("px"), lax.axis_index("py")

    def one(mp, carry):
        for mh in range(3):
            m = mh * 4 + mp
            kx, ky, kz, retained, square, damping, weight = waves_of(m, j, l)
            scale = weight * retained
            v = [[scale * state_ref[c, r, m] for r in range(2)] for c in range(3)]
            wy = [-(kz * v[0][1] - kx * v[2][1]), kz * v[0][0] - kx * v[2][0]]
            wz = [-(kx * v[1][1] - ky * v[0][1]), kx * v[1][0] - ky * v[0][0]]
            inverse = 1.0 / jnp.maximum(square, 1.0)
            fscale = TIME_STEP * retained
            force = [[None, None], [None, None], [None, None]]
            for r in range(2):
                g = [damping * cot_ref[c, r, m] for c in range(3)]
                along = (kx * g[0] + ky * g[1] + kz * g[2]) * inverse
                for c, k in enumerate((kx, ky, kz)):
                    force[c][r] = fscale * (g[c] - k * along)
            for f, (re, im) in enumerate([v[0], v[1], v[2], wy, wz, *force]):
                g, pp = divmod(f * 3 + mh, 8)
                top = jnp.concatenate([re, im], axis=1)
                low = jnp.concatenate([im, -re], axis=1)
                block = jnp.concatenate([top, low], axis=0).astype(BF16)
                row = pl.multiple_of(g * 384 + lax.rem(pp + j, 8) * SLOT, 16)
                s_ref[pl.ds(row, SLOT), :] = block
        for first in range(0, INV_W, 256):
            width = min(256, INV_W - first)
            out = dot(tx_ref[...], s_ref[first : first + width, :], NT)
            for c in range(width // 128):
                for xx in range(4):
                    a32[first // 128 + c, pl.ds(mp * 4 + xx, 64, stride=24), :] = out[
                        xx * 64 : (xx + 1) * 64, c * 128 : (c + 1) * 128
                    ]
        return carry

    lax.fori_loop(0, 4, one, 0)

    def pack(d, carry):
        row = pl.multiple_of(d * 24, 8)
        for c in range(INV_W // 128):
            a_ref[d, :, c * 128 : (c + 1) * 128] = a32[c, pl.ds(row, 16), :].astype(BF16)
        return carry

    lax.fori_loop(0, 64, pack, 0)


def exchange(x_ref, o_ref, send_sem, recv_sem, own_sem):
    px, py = lax.axis_index("px"), lax.axis_index("py")
    me = px * 8 + py

    def peer(k):
        t = lax.rem(me + k, NDEV)
        return t, {"px": t // 8, "py": lax.rem(t, 8)}

    barrier = pltpu.get_barrier_semaphore()

    def greet(k, carry):
        pl.semaphore_signal(barrier, inc=1, device_id=peer(k)[1], device_id_type=MESH)
        return carry

    lax.fori_loop(1, NDEV, greet, 0)
    own = pltpu.make_async_copy(x_ref.at[me], o_ref.at[me], own_sem)
    own.start()
    pl.semaphore_wait(barrier, NDEV - 1)

    def send(k, carry):
        t, where = peer(k)
        pltpu.make_async_remote_copy(
            src_ref=x_ref.at[t],
            dst_ref=o_ref.at[me],
            send_sem=send_sem,
            recv_sem=recv_sem,
            device_id=where,
            device_id_type=MESH,
        ).start()
        return carry

    lax.fori_loop(1, NDEV, send, 0)
    own.wait()
    rest = pl.ds(0, NDEV - 1)
    whole = pltpu.make_async_remote_copy(
        src_ref=x_ref.at[rest],
        dst_ref=o_ref.at[rest],
        send_sem=send_sem,
        recv_sem=recv_sem,
        device_id=peer(1)[1],
        device_id_type=MESH,
    )
    whole.wait_send()
    whole.wait_recv()


def lane_select(lane, v, pick):
    slots = [q for q in range(8) if q * SLOT < (v + 1) * 128 and (q + 1) * SLOT > v * 128]
    value = pick(slots[0])
    for q in slots[1:]:
        value = jnp.where(lane >= float(q * SLOT - v * 128), pick(q), value)
    return value


def cross(a, b):
    return [a[1] * b[2] - a[2] * b[1], a[2] * b[0] - a[0] * b[2], a[0] * b[1] - a[1] * b[0]]


def slab(
    r_ref, ty_ref, tyk_ref, tz_ref, tzk_ref, tzt_ref, tzkt_ref, perm_ref, w_in_t, b_ref, w_out,
    o_ref,
    lhs, y32, v32, va32, l32, o16, win, wint, woutt, gin, gout,
):
    lane = lax.broadcasted_iota(jnp.int32, (1, 128), 1).astype(BF16)
    lane = jnp.broadcast_to(lane, (128, 128))

    perm = perm_ref[...]
    win[...] = dot(w_in_t[...], perm, TN).astype(BF16)
    wint[...] = dot(perm, w_in_t[...], TN).astype(BF16)
    woutt[...] = dot(w_out[...], perm, TN).astype(BF16)

    for pp in range(8):
        first = (8 - pp) * SLOT
        for g in range(3):
            for v in range(3):
                at = g * 384 + v * 128
                lhs[g * 128 : (g + 1) * 128, v * 128 : (v + 1) * 128] = lane_select(
                    lane, v, lambda q: r_ref[(q - pp) % 8, :, at : at + 128]
                )
        out = dot(lhs[...], ty_ref[first : first + 384, :])
        for c in range(4):
            y32[c, pp * 384 : (pp + 1) * 384, :] = out[:, c * 128 : (c + 1) * 128]
        for mh in range(3):
            g, own = divmod(2 * 3 + mh, 8)
            if own == pp:
                out = -dot(lhs[g * 128 : (g + 1) * 128, :], tyk_ref[first : first + 384, :])
                row = 3072 + mh * 128
                for c in range(4):
                    y32[c, row : row + 128, :] = out[:, c * 128 : (c + 1) * 128]

    def block_of(f, mh):
        if f == INV:
            return 24 + mh
        g, pp = divmod(f * 3 + mh, 8)
        return pp * 3 + g

    def columns(f, xx):
        parts = []
        for t in range(2):
            for mh in range(3):
                rows = pl.ds(block_of(f, mh) * 128 + xx, 32, stride=4)
                parts.append(jnp.concatenate([y32[2 * t, rows, :], y32[2 * t + 1, rows, :]], axis=1))
        return jnp.concatenate(parts, axis=0).astype(BF16)

    def along_z(xx, carry):
        for slot, f in enumerate((0, 1, 2, INV, 3, 4, 5, 6, 7)):
            out = dot(tz_ref[...], columns(f, xx))
            if f == INV:
                out = out + dot(tzk_ref[...], columns(1, xx))
            out = out.astype(BF16).astype(F32)
            for dz in range(4):
                row = pl.multiple_of((slot * 16 + xx * 4 + dz) * PITCH, 8)
                for h in range(2):
                    v32[h, pl.ds(row, 64), :] = out[dz * 64 : (dz + 1) * 64, h * 128 : (h + 1) * 128]
        return carry

    lax.fori_loop(0, 4, along_z, 0)

    gin[...] = jnp.zeros_like(gin)
    gout[...] = jnp.zeros_like(gout)
    ones = jnp.ones((64, 256), BF16)

    def rows_of(field, bz):
        rows = pl.ds(field * 16 * PITCH + bz, 48, stride=PITCH)
        return [v32[h, rows, :] for h in range(2)]

    def boxes(planes):
        parts = []
        for dy in range(4):
            h, at = dy // 2, dy % 2 * 64
            parts.append(jnp.concatenate([p[h][:, at : at + 64] for p in planes], axis=1))
        return jnp.concatenate(parts, axis=0).astype(BF16)

    def closure(group, carry):
        bzs = [group * 4 + b for b in range(4)]
        velocity = [rows_of(0, bz) for bz in bzs]
        force = [rows_of(6, bz) for bz in bzs]
        features = boxes(velocity)
        adjoints = boxes(force)
        pre = dot(win[...], features) + b_ref[...]
        sigmoid = 1.0 / (1.0 + jnp.exp(-pre))
        hidden = (pre * sigmoid).astype(BF16)
        hidden_adj = FORCING * dot(woutt[...], adjoints)
        pre_adj = (hidden_adj * sigmoid * (1.0 + pre * (1.0 - sigmoid))).astype(BF16)
        gin[...] += dot(pre_adj, jnp.concatenate([features, ones], axis=0), NT)
        gout[:, 0:FEAT] += dot(hidden, adjoints, NT)
        feat_adj = dot(wint[...], pre_adj)
        for b, bz in enumerate(bzs):
            spin = rows_of(3, bz)
            for h in range(2):
                back = jnp.concatenate(
                    [feat_adj[dy * 48 : (dy + 1) * 48, b * 64 : (b + 1) * 64] for dy in (2 * h, 2 * h + 1)], axis=1
                )
                pick = lambda a: [a[c * 16 : (c + 1) * 16, :] for c in range(3)]
                vel, vor, frc = pick(velocity[b][h]), pick(spin[h]), pick(force[b][h])
                first = jnp.concatenate(cross(vor, frc), axis=0) + back
                second = jnp.concatenate(cross(frc, vel), axis=0)
                va32[h, pl.ds(bz, 48, stride=PITCH), :] = first
                va32[h, pl.ds(48 * PITCH + bz, 48, stride=PITCH), :] = second
        return carry

    lax.fori_loop(0, 16, closure, 0)

    def field_of(c, xx):
        parts = []
        for dz in range(4):
            row = pl.multiple_of((c * 16 + xx * 4 + dz) * PITCH, 8)
            parts.append(jnp.concatenate([va32[0, pl.ds(row, 64), :], va32[1, pl.ds(row, 64), :]], axis=1))
        return jnp.concatenate(parts, axis=0).astype(BF16)

    def put(block, value, xx):
        for r in range(2):
            for mh in range(3):
                for h in range(2):
                    l32[2 * r + h, pl.ds(block(mh) * 128 + xx, 32, stride=4), :] = value[
                        r * 96 + mh * 32 : r * 96 + (mh + 1) * 32, h * 128 : (h + 1) * 128
                    ]

    def main(f):
        def block(mh):
            g, pp = divmod(f * 3 + mh, 8)
            return pp * 2 + g
        return block

    def extra(f):
        return lambda mh: 16 + f * 3 + mh

    def forward_z(xx, carry):
        vort = field_of(4, xx)
        tzt = tzt_ref[...]
        tzkt = tzkt_ref[...]
        put(main(0), dot(tzt, field_of(0, xx)) - dot(tzkt, vort), xx)
        put(main(3), dot(tzt, vort), xx)
        vort = field_of(3, xx)
        put(main(2), dot(tzt, field_of(1, xx)) + dot(tzkt, vort), xx)
        put(extra(1), -dot(tzt, vort), xx)
        put(main(1), dot(tzt, field_of(2, xx)), xx)
        value = dot(tzt, field_of(5, xx))
        put(main(4), value, xx)
        put(extra(0), value, xx)
        return carry

    for c in range(4):
        l32[c, 15 * 128 : 16 * 128, :] = jnp.zeros((128, 128), F32)
    lax.fori_loop(0, 4, forward_z, 0)

    for pp in range(8):
        first = (8 - pp) * SLOT
        rows = slice(pp * 256, (pp + 1) * 256)
        left = jnp.concatenate([l32[c, rows, :] for c in range(4)], axis=1).astype(BF16)
        out = dot(left, ty_ref[first : first + 384, :], NT)
        if pp < 6:
            rows = slice((16 + pp) * 128, (17 + pp) * 128)
            left = jnp.concatenate([l32[c, rows, :] for c in range(4)], axis=1).astype(BF16)
            more = dot(left, tyk_ref[first : first + 384, :], NT)
            o16[pp, 0:128, :] = (out[0:128] + more).astype(BF16)
            o16[pp, 128:256, :] = out[128:256].astype(BF16)
        else:
            o16[pp] = out.astype(BF16)
    for j in range(8):
        for g in range(2):
            for v in range(3):
                at = g * 384 + v * 128
                o_ref[j, :, at : at + 128] = lane_select(
                    lane, v, lambda q: o16[(q - j) % 8, g * 128 : (g + 1) * 128, v * 128 : (v + 1) * 128]
                )
    for j in range(8):
        rows = slice(j * 64, (j + 1) * 64)
        both = jnp.concatenate([gin[rows, :].reshape(8, 8, 256), (FORCING * gout[rows, :]).reshape(8, 8, 256)], axis=1)
        o_ref[j, :, FWD_W:SEND_W] = both.reshape(128, 256).astype(BF16)


def spectral_in(q_ref, cot_ref, tx_ref, back_ref, out_ref, grad_ref, q32, o32):
    j, l = lax.axis_index("px"), lax.axis_index("py")

    def unpack(d, total):
        row = pl.multiple_of(d * 24, 8)
        for c in range(FWD_W // 128):
            q32[c, pl.ds(row, 16), :] = q_ref[d, :, c * 128 : (c + 1) * 128].astype(F32)
        return total + q_ref[d, :, FWD_W:SEND_W].astype(F32)

    total = lax.fori_loop(0, 64, unpack, jnp.zeros((16, 256), F32))
    grad_ref[...] = dot(total, back_ref[...], precision=lax.Precision.HIGHEST)

    def one(mp, carry):
        for c in range(FWD_W // 128):
            left = jnp.concatenate([q32[c, pl.ds(mp * 4 + xx, 64, stride=24), :] for xx in range(4)], axis=0)
            o32[c * 128 : (c + 1) * 128, :] = dot(left.astype(BF16), tx_ref[...], TN)
        for mh in range(3):
            m = mh * 4 + mp
            kx, ky, kz, retained, square, damping, weight = waves_of(m, j, l)
            scale = weight * retained
            parts = []
            for f in range(5):
                g, pp = divmod(f * 3 + mh, 8)
                row = pl.multiple_of(g * 384 + lax.rem(pp + j, 8) * SLOT, 8)
                re = o32[pl.ds(row, WY), :]
                im = o32[pl.ds(row + WY, WY), :]
                parts.append((re[:, :NG] - im[:, NG:], im[:, :NG] + re[:, NG:]))
            ax, az, ay, wy, wz = parts
            spec = [
                ax,
                (ay[0] + kx * wz[1], ay[1] - kx * wz[0]),
                (az[0] - kx * wy[1], az[1] + kx * wy[0]),
            ]
            for c in range(3):
                for r in range(2):
                    out_ref[c, r, m] = damping * cot_ref[c, r, m] + scale * spec[c][r]
        return carry

    lax.fori_loop(0, 4, one, 0)


VMEM = pl.BlockSpec(memory_space=pltpu.VMEM)
ANY = pl.BlockSpec(memory_space=pl.ANY)
LIMIT = 60 * 1024 * 1024


def call(body, outs, ins, scratch, **params):
    return pl.pallas_call(
        body,
        out_shape=outs,
        in_specs=[VMEM] * ins,
        out_specs=jax.tree.map(lambda _: VMEM, outs),
        scratch_shapes=scratch,
        compiler_params=pltpu.CompilerParams(vmem_limit_bytes=LIMIT, **params),
    )


def all_to_all(x, number):
    return pl.pallas_call(
        exchange,
        out_shape=jax.ShapeDtypeStruct(x.shape, x.dtype),
        in_specs=[ANY],
        out_specs=ANY,
        scratch_shapes=[pltpu.SemaphoreType.DMA] * 3,
        compiler_params=pltpu.CompilerParams(collective_id=number, has_side_effects=True),
    )(x)


def shards(state, cotangent, w_in, b_in, w_out):
    t = {k: jnp.asarray(v) for k, v in make_tables().items()}
    state = state.transpose(0, 1, 3, 2, 4)
    cotangent = cotangent.transpose(0, 1, 3, 2, 4)
    sds = jax.ShapeDtypeStruct
    sent = call(
        spectral_out,
        sds((NDEV, 16, INV_W), BF16),
        3,
        [pltpu.VMEM((INV_W, 2 * NG), BF16), pltpu.VMEM((INV_W // 128, 64 * 24, 128), F32)],
    )(state, cotangent, t["tx"])
    got = all_to_all(sent, 0).reshape(8, 128, INV_W)
    back = call(
        slab,
        sds((8, 128, SEND_W), BF16),
        11,
        [
            pltpu.VMEM((384, 384), BF16),
            pltpu.VMEM((4, 27 * 128, 128), F32),
            pltpu.VMEM((2, 144 * PITCH, 128), F32),
            pltpu.VMEM((2, 96 * PITCH, 128), F32),
            pltpu.VMEM((4, 22 * 128, 128), F32),
            pltpu.VMEM((8, 256, 384), BF16),
            pltpu.VMEM((HID, FEAT), BF16),
            pltpu.VMEM((FEAT, HID), BF16),
            pltpu.VMEM((HID, FEAT), BF16),
            pltpu.VMEM((HID, 256), F32),
            pltpu.VMEM((HID, 256), F32),
        ],
    )(
        got, t["ty"], t["tyk"], t["tz"], t["tzk"], t["tzt"], t["tzkt"], t["perm"],
        w_in.T, b_in[:, None], w_out,
    )
    mine = all_to_all(back.reshape(NDEV, 16, SEND_W), 1)
    grad, sums = call(
        spectral_in,
        (sds((3, 2, WZ, WY, NG), F32), sds((16, 256), F32)),
        4,
        [pltpu.VMEM((FWD_W // 128, 64 * 24, 128), F32), pltpu.VMEM((FWD_W, 2 * NG), F32)],
    )(mine, cotangent, t["tx"], t["back"])
    return (
        grad.transpose(0, 1, 3, 2, 4),
        sums[0:8, 0:FEAT],
        sums[8:16, 0:FEAT].T,
        sums[0:8, FEAT][None, :],
    )


def solution(mesh):
    split = P("rep", None, "px", "py", None)
    both = ("px", "py")
    return jax.shard_map(
        shards,
        mesh=mesh,
        in_specs=(split, split, P(), P(), P()),
        out_specs=(split, P(both, "rep"), P("rep", both), P("rep", both)),
        check_vma=False,
    )
```

profile of v0, /device:TPU:1, one launch (start us, length us, event | category | flops | bytes accessed | tf_op | source)
XLA Modules:
  0.0 116.9 jit_solution(12385757140549025432)
XLA Ops:
  0.6 7.6 %shard_map.165.x_ref = bf16[64,16,1152]{2,1,0:T(8,128)(2,1)} custom-call(f32[3,2,12,24,256]{4,3,2,1,0:T(8,128)} %bitcast.14, f32[3,2,12,24,256]{4,3,2,1,0:T(8,128)} %bitcast.12, bf16[256,512]{1,0:T(8,128)(2,1)} %constant.18.clone.tx_ref), custom_call_target="tpu_custom_call" | custom-call | tf_op jit(solution)/shard_map/pallas_call | solution.py:440
  8.3 0.0 copy-start
  8.3 38.3 %shard_map.166 = bf16[64,16,1152]{2,1,0:T(8,128)(2,1)} custom-call(bf16[64,16,1152]{2,1,0:T(8,128)(2,1)} %shard_map.165.x_ref), custom_call_target="tpu_custom_call" | custom-call | tf_op jit(solution)/shard_map/pallas_call | solution.py:425
  46.6 0.0 copy-done
  46.6 0.9 copy.18.b_ref
  47.4 26.5 %shard_map.167 = bf16[8,128,1024]{2,1,0:T(8,128)(2,1)} custom-call(bf16[8,128,1152]{2,1,0:T(8,128)(2,1)} %bitcast.10, bf16[768,512]{1,0:T(8,128)(2,1)} %constant.19.clone.ty_ref, bf16[768,512]{1,0:T(8,128)(2,1)} %constant.20.clone.tyk_ref, bf16[256,192]{1,0:T(8,128)(2,1)} %constant.21.clone.tz_ref, bf16[256,192]{1,0:T(8,128)(2,1)} %constant.22.clone.tzk_ref, ...), custom_call_target="tpu_custom_call" | custom-call | tf_op jit(solution)/shard_map/pallas_call | solution.py:447
  73.9 34.1 %shard_map.168.q_ref = bf16[64,16,1024]{2,1,0:T(8,128)(2,1)} custom-call(bf16[64,16,1024]{2,1,0:T(8,128)(2,1)} %bitcast.11), custom_call_target="tpu_custom_call" | custom-call | tf_op jit(solution)/shard_map/pallas_call | solution.py:425
  108.0 6.2 %shard_map.169 = (f32[3,2,12,24,256]{4,3,2,1,0:T(8,128)}, f32[16,256]{1,0:T(8,128)}) custom-call(bf16[64,16,1024]{2,1,0:T(8,128)(2,1)} %shard_map.168.q_ref, f32[3,2,12,24,256]{4,3,2,1,0:T(8,128)} %bitcast.13, bf16[256,512]{1,0:T(8,128)(2,1)} %constant.18.clone.tx_ref, f32[256,256]{1,0:T(8,128)} %constant.26.clone.back_ref), custom_call_target="tpu_custom_call" | custom-call | tf_op jit(solution)/shard_map/pallas_call | solution.py:469
  114.2 1.3 %slice_bitcast_fusion = (f32[192,8]{0,1:T(8,128)}, f32[8,192]{1,0:T(8,128)}) fusion(f32[16,256]{1,0:T(8,128)} %get-tuple-element.7), kind=kLoop, calls=%fused_computation | loop fusion | bytes 24576 | tf_op jit(solution)/shard_map/transpose | solution.py:478
  115.5 1.4 %slice_reduce_fusion = f32[8]{0:T(128)} fusion(f32[16,256]{1,0:T(8,128)} %get-tuple-element.7), kind=kLoop, calls=%fused_computation.1 | loop fusion | bytes 64 | tf_op jit(solution)/shard_map/slice | solution.py:479
Async XLA Ops:
  8.3 38.3 %copy-start = (f32[512]{0:T(512)S(1)}, f32[512]{0:T(512)}, u32[]{:S(2)}) copy-start(f32[512]{0:T(512)} %param.17) | copy-start | bytes 6148
where the time goes:
time: 118 us; the launch traced here: 117 us
  Pallas kernels  113 us (96%)
  local copies, waits for them, and re-layouts  3.55 us (3%)
    pallas_call x2, Pallas kernels, all_to_all(): pl.pallas_call(exchange, out_shape=jax.ShapeDtypeStruct(x.shape, x.dtype)...  72.3 us
    pallas_call x1, Pallas kernels, shards(): call(slab, sds((8, 128, SEND_W), BF16), 11, [pltpu.VMEM((384, 384), BF16)...  26.5 us
    pallas_call x1, Pallas kernels, shards(): call(spectral_out, sds((NDEV, 16, INV_W), BF16), 3, [pltpu.VMEM((INV_W, 2...  7.63 us
    pallas_call x1, Pallas kernels, shards(): call(spectral_in, (sds((3, 2, WZ, WY, NG), F32), sds((16, 256), F32)), 4,...  6.24 us

commit v1 on v0

v1 whole, which is shorter than its diff:
```python
import numpy as np

import jax
import jax.numpy as jnp
from jax import lax
from jax.experimental import pallas as pl
from jax.experimental.pallas import tpu as pltpu
from jax.sharding import PartitionSpec as P

F32 = jnp.float32
BF16 = jnp.bfloat16
MESH = pl.DeviceIdType.MESH
NN = (((1,), (0,)), ((), ()))
NT = (((1,), (1,)), ((), ()))
TN = (((0,), (0,)), ((), ()))

NG, KY, KZ, HID, FEAT = 256, 192, 96, 512, 192
CUT = NG // 3
NU_DT = 5e-05
TIME_STEP = 0.01
FORCING = 20.0
NDEV = 64
WY, WZ = 24, 12
SLOT = 48
ROW = 8 * SLOT
INV = 8
FWD = 2
PITCH = 72


def dot(a, b, dims=NN, **kw):
    return lax.dot_general(a, b, dims, preferred_element_type=F32, **kw)


def make_tables():
    bf = jnp.bfloat16

    def angle(k, x):
        theta = 2 * np.pi * ((np.asarray(k)[:, None] % NG) * np.asarray(x)[None, :] % NG) / NG
        return np.cos(theta) / np.sqrt(NG), np.sin(theta) / np.sqrt(NG)

    order_x = np.arange(NG).reshape(64, 4).T.reshape(-1)
    c, s = angle(order_x, np.arange(NG))
    tx = np.concatenate([c, -s], axis=1)
    order = np.arange(NG).reshape(64, 4).T.reshape(-1)
    ids = np.arange(KY)
    ky = np.where(ids < KY // 2, ids, ids - KY)
    c, s = angle(ky, order)
    top = np.concatenate([c, s], axis=1).reshape(8, 1, WY, 2 * NG)
    low = np.concatenate([-s, c], axis=1).reshape(8, 1, WY, 2 * NG)
    kcol = ky.reshape(8, 1, WY, 1)
    ty = np.concatenate([top, low], axis=1).reshape(2 * KY, 2 * NG)
    tyk = np.concatenate([-kcol * low, kcol * top], axis=1).reshape(2 * KY, 2 * NG)
    kz = (np.arange(8)[None, :, None] * WZ + np.arange(3)[:, None, None] * 4 + np.arange(4)[None, None, :]).reshape(-1)
    c, s = angle(order, kz)
    tz = np.concatenate([c, -s], axis=1)
    kk = np.concatenate([kz, kz])[None, :]
    tzk = np.concatenate([s, c], axis=1) * kk
    perm = np.zeros((FEAT, FEAT), np.float32)
    src = np.arange(FEAT).reshape(3, 4, 4, 4).transpose(2, 0, 1, 3).reshape(-1)
    perm[src, np.arange(FEAT)] = 1.0
    back = np.zeros((256, 256), np.float32)
    back[:FEAT, :FEAT] = perm.T
    back[FEAT, FEAT] = 1.0
    arrays = dict(tx=tx, ty=ty, tyk=tyk, tz=tz, tzk=tzk, tzt=tz.T, tzkt=tzk.T, perm=perm)
    out = {k: np.asarray(v, np.float32).astype(bf) for k, v in arrays.items()}
    out["back"] = back
    return out


def waves_of(m, j, l):
    kz_id = l * WZ + m
    kz = kz_id.astype(F32)
    a = lax.broadcasted_iota(jnp.int32, (WY, NG), 0) + j * WY
    n = lax.broadcasted_iota(jnp.int32, (WY, NG), 1)
    ky = jnp.where(a < KY // 2, a, a - KY).astype(F32)
    kx = jnp.where(n < NG // 2, n, n - NG).astype(F32)
    keep = (jnp.abs(kx) <= CUT) & (jnp.abs(ky) <= CUT) & (kz <= float(CUT))
    retained = keep.astype(F32)
    square = kx * kx + ky * ky + kz * kz
    damping = jnp.exp(-NU_DT * square)
    weight = jnp.where(kz_id == 0, 1.0, 2.0).astype(F32)
    return kx, ky, kz, retained, square, damping, weight


PART = 24
GRADS = INV * 3 // 8


def lane_select(lane, v, pick):
    slots = [q for q in range(8) if q * SLOT < (v + 1) * 128 and (q + 1) * SLOT > v * 128]
    value = pick(slots[0])
    for q in slots[1:]:
        value = jnp.where(lane >= float(q * SLOT - v * 128), pick(q), value)
    return value


def cross(a, b):
    return [a[1] * b[2] - a[2] * b[1], a[2] * b[0] - a[0] * b[2], a[0] * b[1] - a[1] * b[0]]


def main_kernel(
    state_ref, cot_ref, tx_ref, tz_ref, tzk_ref, tzt_ref, tzkt_ref, perm_ref, back_ref, w_in_t, b_ref, w_out,
    ty_hbm, tyk_hbm,
    out_ref, grad_ref,
    s_ref, flat, sent, got, v32, va32, l32, o16, back, mine, gsent, ggot, o32, ty_ref, tyk_ref,
    win, wint, woutt, gin, gout, table_sem, send_sem, recv_sem,
):
    j, l = lax.axis_index("px"), lax.axis_index("py")
    me = j * 8 + l
    x, core, z, y = j // 2, lax.rem(j, 2), l // 4, lax.rem(l, 4)

    def peer(k):
        k = k + jnp.where(k >= 11, 1, 0)
        i = lax.rem(k, 4)
        dx = jnp.where(i == 0, 1, jnp.where(i == 1, 3, jnp.where(i == 2, 2, 0)))
        dy = jnp.where(i == 0, 1, jnp.where(i == 1, 3, jnp.where(i == 2, 0, 2))) + lax.rem(k // 4, 4)
        tx = lax.rem(x + dx, 4)
        ty = lax.rem(y + dy, 4)
        tc = lax.rem(core + k // 16, 2)
        tz = lax.rem(z + k // 32, 2)
        px, py = tx * 2 + tc, tz * 4 + ty
        return px * 8 + py, {"px": px, "py": py}

    barrier = pltpu.get_barrier_semaphore()

    def greet(k, carry):
        pl.semaphore_signal(barrier, inc=1, device_id=peer(k)[1], device_id_type=MESH)
        return carry

    lax.fori_loop(0, NDEV - 1, greet, 0)
    half = 2 * KY
    loads = [
        pltpu.make_async_copy(src, dst.at[pl.ds(n * half, half)], table_sem.at[k * 2 + n])
        for k, (src, dst) in enumerate([(ty_hbm, ty_ref), (tyk_hbm, tyk_ref)])
        for n in range(2)
    ]
    for load in loads:
        load.start()

    def copy(src, dst, number, where):
        return pltpu.make_async_remote_copy(
            src_ref=src,
            dst_ref=dst,
            send_sem=send_sem.at[number],
            recv_sem=recv_sem.at[number],
            device_id=where,
            device_id_type=MESH,
        )

    def send_all(src, dst, number):
        def send(k, carry):
            t, where = peer(k)
            copy(src.at[t], dst.at[me], number, where).start()
            return carry

        dst[pl.ds(me, 1)] = src[pl.ds(me, 1)]
        lax.fori_loop(0, NDEV - 1, send, 0)

    def whole(src, dst, number):
        rest = pl.ds(0, NDEV - 1)
        return copy(src.at[rest], dst.at[rest], number, peer(0)[1])

    for group in range(3):

        def one(mp, carry):
            for mh in range(3):
                fields = [f for f in range(INV) if (f * 3 + mh) // 8 == group]
                m = mh * 4 + mp
                kx, ky, kz, retained, square, damping, weight = waves_of(m, j, l)
                value = {}
                if any(f >= 3 for f in fields):
                    scale = weight * retained
                    v = [[scale * state_ref[c, r, m] for r in range(2)] for c in range(3)]
                    value.update({3 + c: v[c] for c in range(3)})
                    value[6] = [-(kz * v[0][1] - kx * v[2][1]), kz * v[0][0] - kx * v[2][0]]
                    value[7] = [-(kx * v[1][1] - ky * v[0][1]), kx * v[1][0] - ky * v[0][0]]
                if any(f < 3 for f in fields):
                    inverse = 1.0 / jnp.maximum(square, 1.0)
                    scale = TIME_STEP * retained
                    force = [[], [], []]
                    for r in range(2):
                        w = [damping * cot_ref[c, r, m] for c in range(3)]
                        along = (kx * w[0] + ky * w[1] + kz * w[2]) * inverse
                        for c, k in enumerate((kx, ky, kz)):
                            force[c].append(scale * (w[c] - k * along))
                    value.update({c: force[c] for c in range(3)})
                for f in fields:
                    re, im = value[f]
                    top = jnp.concatenate([re, im], axis=1)
                    low = jnp.concatenate([im, -re], axis=1)
                    row = pl.multiple_of(lax.rem((f * 3 + mh) % 8 + j, 8) * SLOT, 16)
                    s_ref[pl.ds(row, SLOT), :] = jnp.concatenate([top, low], axis=0).astype(BF16)
            for first in range(0, ROW, 256):
                width = min(256, ROW - first)
                out = dot(tx_ref[...], s_ref[first : first + width, :], NT)
                for c in range(width // 128):
                    for xx in range(4):
                        base = (first // 128 + c) * NDEV * PART
                        flat[pl.ds(base + mp * 4 + xx, NDEV, stride=PART), :] = out[
                            xx * 64 : (xx + 1) * 64, c * 128 : (c + 1) * 128
                        ]
            return carry

        lax.fori_loop(0, 4, one, 0)

        def pack(d, carry):
            for c in range(3):
                row = pl.multiple_of(c * NDEV * PART + d * PART, 8)
                sent[group, d, :, c * 128 : (c + 1) * 128] = flat[pl.ds(row, 16), :].astype(BF16)
            return carry

        lax.fori_loop(0, NDEV, pack, 0, unroll=4)
        if group == 0:
            pl.semaphore_wait(barrier, NDEV - 1)
        send_all(sent.at[group], got.at[group], group)

    lane = lax.broadcasted_iota(jnp.int32, (1, 128), 1).astype(BF16)
    lane = jnp.broadcast_to(lane, (128, 128))

    perm = perm_ref[...]
    win[...] = dot(w_in_t[...], perm, TN).astype(BF16)
    wint[...] = dot(perm, w_in_t[...], TN).astype(BF16)
    woutt[...] = dot(w_out[...], perm, TN).astype(BF16)
    gin[...] = jnp.zeros_like(gin)
    gout[...] = jnp.zeros_like(gout)
    for c in range(4):
        l32[(c * 22 + 15) * 128 : (c * 22 + 16) * 128, :] = jnp.zeros((128, 128), F32)
    for load in loads:
        load.wait()

    BLOCKS = 27

    def along_y(group):
        for pp in range(8):
            first = (8 - pp) * SLOT
            parts = []
            for v in range(3):
                pick = lambda q: got[group, (q - pp) % 8 * 8 : (q - pp) % 8 * 8 + 8, :, v * 128 : (v + 1) * 128].reshape(128, 128)
                parts.append(lane_select(lane, v, pick))
            left = jnp.concatenate(parts, axis=1)
            todo = [(pp * 3 + group, dot(left, ty_ref[first : first + 2 * KY, :]))]
            f, mh = divmod(group * 8 + pp, 3)
            if f == 5:
                todo.append((24 + mh, -dot(left, tyk_ref[first : first + 2 * KY, :])))
            for block, out in todo:
                for c in range(4):
                    row = (c * BLOCKS + block) * 128
                    flat[row : row + 128, :] = out[:, c * 128 : (c + 1) * 128]

    def columns(f, xx):
        parts = []
        for t in range(2):
            for mh in range(3):
                g, pp = divmod(f * 3 + mh, 8)
                block = 24 + mh if f == INV else pp * 3 + g
                lanes = [
                    flat[pl.ds(((2 * t + h) * BLOCKS + block) * 128 + xx, 32, stride=4), :] for h in range(2)
                ]
                parts.append(jnp.concatenate(lanes, axis=1))
        return jnp.concatenate(parts, axis=0).astype(BF16)

    def along_z(fields):
        def one(xx, carry):
            for slot, f in fields:
                out = dot(tz_ref[...], columns(f, xx))
                if f == INV:
                    out = out + dot(tzk_ref[...], columns(4, xx))
                out = out.astype(BF16).astype(F32)
                for dz in range(4):
                    row = pl.multiple_of((slot * 16 + xx * 4 + dz) * PITCH, 8)
                    for h in range(2):
                        v32[h, pl.ds(row, 64), :] = out[dz * 64 : (dz + 1) * 64, h * 128 : (h + 1) * 128]
            return carry

        lax.fori_loop(0, 4, one, 0)

    for group, fields in enumerate([[(6, 0), (7, 1)], [(8, 2), (0, 3), (1, 4)], [(2, 5), (3, INV), (4, 6), (5, 7)]]):
        whole(sent.at[group], got.at[group], group).wait_recv()
        along_y(group)
        along_z(fields)

    ones = jnp.ones((64, 256), BF16)

    def rows_of(field, bz):
        rows = pl.ds(field * 16 * PITCH + bz, 48, stride=PITCH)
        return [v32[h, rows, :] for h in range(2)]

    def boxes(planes):
        parts = []
        for dy in range(4):
            h, at = dy // 2, dy % 2 * 64
            parts.append(jnp.concatenate([p[h][:, at : at + 64] for p in planes], axis=1))
        return jnp.concatenate(parts, axis=0).astype(BF16)

    def closure(group, carry):
        bzs = [group * 4 + b for b in range(4)]
        velocity = [rows_of(0, bz) for bz in bzs]
        force = [rows_of(6, bz) for bz in bzs]
        features = boxes(velocity)
        adjoints = boxes(force)
        pre = dot(win[...], features) + b_ref[...]
        sigmoid = 1.0 / (1.0 + jnp.exp(-pre))
        hidden = (pre * sigmoid).astype(BF16)
        hidden_adj = FORCING * dot(woutt[...], adjoints)
        pre_adj = (hidden_adj * sigmoid * (1.0 + pre * (1.0 - sigmoid))).astype(BF16)
        gin[...] += dot(pre_adj, jnp.concatenate([features, ones], axis=0), NT)
        gout[:, 0:FEAT] += dot(hidden, adjoints, NT)
        feat_adj = dot(wint[...], pre_adj)
        for b, bz in enumerate(bzs):
            spin = rows_of(3, bz)
            for h in range(2):
                lanes = [feat_adj[dy * 48 : (dy + 1) * 48, b * 64 : (b + 1) * 64] for dy in (2 * h, 2 * h + 1)]
                pick = lambda a: [a[c * 16 : (c + 1) * 16, :] for c in range(3)]
                vel, vor, frc = pick(velocity[b][h]), pick(spin[h]), pick(force[b][h])
                first = jnp.concatenate(cross(vor, frc), axis=0) + jnp.concatenate(lanes, axis=1)
                second = jnp.concatenate(cross(frc, vel), axis=0)
                va32[h, pl.ds(bz, 48, stride=PITCH), :] = first
                va32[h, pl.ds(48 * PITCH + bz, 48, stride=PITCH), :] = second
        return carry

    lax.fori_loop(0, 16, closure, 0)

    def slices(d, carry):
        rows = pl.ds(pl.multiple_of(d * 8, 8), 8)
        gsent[d] = jnp.concatenate([gin[rows, :], FORCING * gout[rows, :]], axis=0).astype(BF16)
        return carry

    lax.fori_loop(0, NDEV, slices, 0, unroll=4)
    send_all(gsent, ggot, GRADS)

    def field_of(c, xx):
        parts = []
        for dz in range(4):
            row = pl.multiple_of((c * 16 + xx * 4 + dz) * PITCH, 8)
            parts.append(jnp.concatenate([va32[0, pl.ds(row, 64), :], va32[1, pl.ds(row, 64), :]], axis=1))
        return jnp.concatenate(parts, axis=0).astype(BF16)

    def put(block, value, xx):
        for r in range(2):
            for mh in range(3):
                for h in range(2):
                    row = ((2 * r + h) * 22 + block(mh)) * 128 + xx
                    l32[pl.ds(row, 32, stride=4), :] = value[
                        r * 96 + mh * 32 : r * 96 + (mh + 1) * 32, h * 128 : (h + 1) * 128
                    ]

    def direct(f):
        def block(mh):
            g, pp = divmod(f * 3 + mh, 8)
            return pp * 2 + g

        return block

    def extra(f):
        return lambda mh: 16 + f * 3 + mh

    def forward_z(xx, carry):
        vort = field_of(4, xx)
        tzt = tzt_ref[...]
        tzkt = tzkt_ref[...]
        put(direct(0), dot(tzt, field_of(0, xx)) - dot(tzkt, vort), xx)
        put(direct(3), dot(tzt, vort), xx)
        vort = field_of(3, xx)
        put(direct(2), dot(tzt, field_of(1, xx)) + dot(tzkt, vort), xx)
        put(extra(1), -dot(tzt, vort), xx)
        put(direct(1), dot(tzt, field_of(2, xx)), xx)
        value = dot(tzt, field_of(5, xx))
        put(direct(4), value, xx)
        put(extra(0), value, xx)
        return carry

    lax.fori_loop(0, 4, forward_z, 0)

    def left_of(block, count):
        parts = [l32[(c * 22 + block) * 128 : (c * 22 + block + count) * 128, :] for c in range(4)]
        return jnp.concatenate(parts, axis=1).astype(BF16)

    for pp in range(8):
        first = (8 - pp) * SLOT
        out = dot(left_of(pp * 2, 2), ty_ref[first : first + 2 * KY, :], NT)
        if pp < 6:
            more = dot(left_of(16 + pp, 1), tyk_ref[first : first + 2 * KY, :], NT)
            o16[pp, 0:128, :] = (out[0:128] + more).astype(BF16)
            o16[pp, 128:256, :] = out[128:256].astype(BF16)
        else:
            o16[pp] = out.astype(BF16)
    for g in range(FWD):
        for to in range(8):
            for v in range(3):
                pick = lambda q: o16[(q - to) % 8, g * 128 : (g + 1) * 128, v * 128 : (v + 1) * 128]
                back[g, to * 8 : to * 8 + 8, :, v * 128 : (v + 1) * 128] = lane_select(lane, v, pick).reshape(8, 16, 128)
        send_all(back.at[g], mine.at[g], GRADS + 1 + g)

    whole(gsent, ggot, GRADS).wait_recv()
    total = lax.fori_loop(0, NDEV, lambda d, t: t + ggot[d].astype(F32), jnp.zeros((16, 256), F32), unroll=4)
    grad_ref[...] = dot(total, back_ref[...], precision=lax.Precision.HIGHEST)

    for g in range(FWD):
        whole(back.at[g], mine.at[g], GRADS + 1 + g).wait_recv()

        def unpack(d, carry):
            for c in range(3):
                row = pl.multiple_of(((g * 3 + c) * NDEV + d) * PART, 8)
                flat[pl.ds(row, 16), :] = mine[g, d, :, c * 128 : (c + 1) * 128].astype(F32)
            return carry

        lax.fori_loop(0, NDEV, unpack, 0, unroll=4)

        def along_x(mp, carry):
            for c in range(3):
                rows = [
                    flat[pl.ds((g * 3 + c) * NDEV * PART + mp * 4 + xx, NDEV, stride=PART), :] for xx in range(4)
                ]
                left = jnp.concatenate(rows, axis=0).astype(BF16)
                o32[mp, (g * 3 + c) * 128 : (g * 3 + c + 1) * 128, :] = dot(left, tx_ref[...], TN)
            return carry

        lax.fori_loop(0, 4, along_x, 0)

    def finish(mp, carry):
        for mh in range(3):
            m = mh * 4 + mp
            kx, ky, kz, retained, square, damping, weight = waves_of(m, j, l)
            scale = weight * retained
            parts = []
            for f in range(5):
                g, pp = divmod(f * 3 + mh, 8)
                row = pl.multiple_of(g * ROW + lax.rem(pp + j, 8) * SLOT, 8)
                re = o32[mp, pl.ds(row, WY), :]
                im = o32[mp, pl.ds(row + WY, WY), :]
                parts.append((re[:, :NG] - im[:, NG:], im[:, :NG] + re[:, NG:]))
            ax, az, ay, wy, wz = parts
            spec = [
                ax,
                (ay[0] + kx * wz[1], ay[1] - kx * wz[0]),
                (az[0] - kx * wy[1], az[1] + kx * wy[0]),
            ]
            for c in range(3):
                for r in range(2):
                    out_ref[c, r, m] = damping * cot_ref[c, r, m] + scale * spec[c][r]
        return carry

    lax.fori_loop(0, 4, finish, 0)
    for group in range(3):
        whole(sent.at[group], got.at[group], group).wait_send()
    whole(gsent, ggot, GRADS).wait_send()
    for g in range(FWD):
        whole(back.at[g], mine.at[g], GRADS + 1 + g).wait_send()


VMEM = pl.BlockSpec(memory_space=pltpu.VMEM)
ANY = pl.BlockSpec(memory_space=pl.ANY)


def shards(state, cotangent, w_in, b_in, w_out):
    t = {k: jnp.asarray(v) for k, v in make_tables().items()}
    state = state.transpose(0, 1, 3, 2, 4)
    cotangent = cotangent.transpose(0, 1, 3, 2, 4)
    sds = jax.ShapeDtypeStruct
    grad, sums = pl.pallas_call(
        main_kernel,
        out_shape=(sds((3, 2, WZ, WY, NG), F32), sds((16, 256), F32)),
        in_specs=[VMEM] * 12 + [ANY] * 2,
        out_specs=(VMEM, VMEM),
        scratch_shapes=[
            pltpu.VMEM((ROW, 2 * NG), BF16),
            pltpu.VMEM((4 * 27 * 128, 128), F32),
            pltpu.VMEM((3, NDEV, 16, ROW), BF16),
            pltpu.VMEM((3, NDEV, 16, ROW), BF16),
            pltpu.VMEM((2, 144 * PITCH, 128), F32),
            pltpu.VMEM((2, 96 * PITCH, 128), F32),
            pltpu.VMEM((4 * 22 * 128, 128), F32),
            pltpu.VMEM((8, 256, ROW), BF16),
            pltpu.VMEM((FWD, NDEV, 16, ROW), BF16),
            pltpu.VMEM((FWD, NDEV, 16, ROW), BF16),
            pltpu.VMEM((NDEV, 16, 256), BF16),
            pltpu.VMEM((NDEV, 16, 256), BF16),
            pltpu.VMEM((4, FWD * ROW, 2 * NG), F32),
            pltpu.VMEM((4 * KY, 2 * NG), BF16),
            pltpu.VMEM((4 * KY, 2 * NG), BF16),
            pltpu.VMEM((HID, FEAT), BF16),
            pltpu.VMEM((FEAT, HID), BF16),
            pltpu.VMEM((HID, FEAT), BF16),
            pltpu.VMEM((HID, 256), F32),
            pltpu.VMEM((HID, 256), F32),
            pltpu.SemaphoreType.DMA((4,)),
            pltpu.SemaphoreType.DMA((6,)),
            pltpu.SemaphoreType.DMA((6,)),
        ],
        compiler_params=pltpu.CompilerParams(
            collective_id=0, has_side_effects=True, vmem_limit_bytes=64000 * 1024
        ),
    )(
        state, cotangent, t["tx"], t["tz"], t["tzk"], t["tzt"], t["tzkt"], t["perm"], t["back"],
        w_in.T, b_in[:, None], w_out, t["ty"], t["tyk"],
    )
    return (
        grad.transpose(0, 1, 3, 2, 4),
        sums[0:8, 0:FEAT],
        sums[8:16, 0:FEAT].T,
        sums[0:8, FEAT][None, :],
    )


def solution(mesh):
    split = P("rep", None, "px", "py", None)
    both = ("px", "py")
    return jax.shard_map(
        shards,
        mesh=mesh,
        in_specs=(split, split, P(), P(), P()),
        out_specs=(split, P(both, "rep"), P("rep", both), P("rep", both)),
        check_vma=False,
    )
```

time: 118 us -> 97 us (0.82)
  Pallas kernels: 113 us -> 89 us
  local copies, waits for them, and re-layouts: 3.55 us -> 7.1 us
    pallas_call x5 -> x1, Pallas kernels: 113 us -> 89 us  [shards(): pl.pallas_call(main_kernel, out_shape=(sds((3, 2, WZ, WY, NG), F32), sds(...]
    unnamed x2 -> x1, local copies, waits for them, and re-layouts: 0.01 us -> 2.87 us
where the time goes in v1:
time: 97 us; the launch traced here: 96.7 us
  Pallas kernels  89 us (92%)
  local copies, waits for them, and re-layouts  7.1 us (7%)
    pallas_call x1, Pallas kernels, shards(): pl.pallas_call(main_kernel, out_shape=(sds((3, 2, WZ, WY, NG), F32), sds(...  89 us
    unnamed x1, local copies, waits for them, and re-layouts  2.87 us

profile of v1, /device:TPU:1, one launch (start us, length us, event | category | flops | bytes accessed | tf_op | source)
XLA Modules:
  0.0 96.7 jit_solution(18376072161149124400)
XLA Ops:
  0.6 1.5 %copy.18.b_ref = f32[512,1]{1,0:T(8,128)} copy(f32[512,1]{0,1:T(1,128)} %bitcast.12) | data formatting | bytes 4096 | tf_op jit(solution)/shard_map/broadcast_in_dim | solution.py:496
  2.2 89.0 %shard_map.165 = (f32[3,2,12,24,256]{4,3,2,1,0:T(8,128)}, f32[16,256]{1,0:T(8,128)}) custom-call(f32[3,2,12,24,256]{4,3,2,1,0:T(8,128)} %bitcast.8, f32[3,2,12,24,256]{4,3,2,1,0:T(8,128)} %bitcast.9, bf16[256,512]{1,0:T(8,128)(2,1)} %constant.18.clone.tx_ref, bf16[256,192]{1,0:T(8,128)(2,1)} %constant.21.clone.tz_ref, ...), custom_call_target="tpu_custom_call" | custom-call | tf_op jit(solution)/shard_map/pallas_call | solution.py:461
  91.1 1.4 %slice_reduce_fusion = f32[8]{0:T(128)} fusion(f32[16,256]{1,0:T(8,128)} %get-tuple-element.7), kind=kLoop, calls=%fused_computation.1 | loop fusion | bytes 64 | tf_op jit(solution)/shard_map/slice | solution.py:502
  92.5 1.3 %slice_bitcast_fusion = (f32[192,8]{0,1:T(8,128)}, f32[8,192]{1,0:T(8,128)}) fusion(f32[16,256]{1,0:T(8,128)} %get-tuple-element.7), kind=kLoop, calls=%fused_computation | loop fusion | bytes 24576 | tf_op jit(solution)/shard_map/transpose | solution.py:501
  93.8 2.9 %copy.20 = f32[3,2,24,12,256]{4,2,3,1,0:T(8,128)} copy(f32[3,2,24,12,256]{4,2,3,1,0:T(8,128)} %bitcast.10) | data formatting | bytes 3538944

commit v2 on v1

--- a/solution.py
+++ b/solution.py
@@ -83,6 +83,7 @@
     return kx, ky, kz, retained, square, damping, weight
 
 
+LIMIT = 46 * 1024 * 1024
 PART = 24
 GRADS = INV * 3 // 8
 
@@ -100,27 +101,25 @@
 
 
 def main_kernel(
-    state_ref, cot_ref, tx_ref, tz_ref, tzk_ref, tzt_ref, tzkt_ref, perm_ref, back_ref, w_in_t, b_ref, w_out,
+    state_hbm, cot_hbm, tx_hbm, tz_hbm, tzk_hbm, tzt_hbm, tzkt_hbm, perm_hbm, back_hbm, w_in_hbm, b_hbm, w_out_hbm,
     ty_hbm, tyk_hbm,
-    out_ref, grad_ref,
-    s_ref, flat, sent, got, v32, va32, l32, o16, back, mine, gsent, ggot, o32, ty_ref, tyk_ref,
-    win, wint, woutt, gin, gout, table_sem, send_sem, recv_sem,
+    out_ref, grad_in_ref, grad_out_ref, grad_bias_ref,
+    state_ref, cot_ref, tx_ref, tz_ref, tzk_ref, tzt_ref, tzkt_ref, perm_ref, back_ref, w_in_t, b_row, w_out,
+    s_ref, flat, sent, got, v32, va32, o16, back, mine, gsent, ggot, ty_ref, tyk_ref,
+    win, wint, woutt, bias, gin, gout, load_sem, send_sem, recv_sem,
 ):
     j, l = lax.axis_index("px"), lax.axis_index("py")
     me = j * 8 + l
-    x, core, z, y = j // 2, lax.rem(j, 2), l // 4, lax.rem(l, 4)
+    x, core, z, y = j >> 1, j & 1, l >> 2, l & 3
+    l32, o32 = v32, va32
 
     def peer(k):
-        k = k + jnp.where(k >= 11, 1, 0)
-        i = lax.rem(k, 4)
-        dx = jnp.where(i == 0, 1, jnp.where(i == 1, 3, jnp.where(i == 2, 2, 0)))
-        dy = jnp.where(i == 0, 1, jnp.where(i == 1, 3, jnp.where(i == 2, 0, 2))) + lax.rem(k // 4, 4)
-        tx = lax.rem(x + dx, 4)
-        ty = lax.rem(y + dy, 4)
-        tc = lax.rem(core + k // 16, 2)
-        tz = lax.rem(z + k // 32, 2)
-        px, py = tx * 2 + tc, tz * 4 + ty
-        return px * 8 + py, {"px": px, "py": py}
+        k = k + jnp.where(k >= 3, 1, 0)
+        dx = (k & 3) + 1
+        dy = dx + ((k >> 2) & 3)
+        px = (((x + dx) & 3) << 1) + ((core + (k >> 4)) & 1)
+        py = (((z + (k >> 5)) & 1) << 2) + ((y + dy) & 3)
+        return (px << 3) + py, {"px": px, "py": py}
 
     barrier = pltpu.get_barrier_semaphore()
 
@@ -128,15 +127,16 @@
         pl.semaphore_signal(barrier, inc=1, device_id=peer(k)[1], device_id_type=MESH)
         return carry
 
-    lax.fori_loop(0, NDEV - 1, greet, 0)
     half = 2 * KY
-    loads = [
-        pltpu.make_async_copy(src, dst.at[pl.ds(n * half, half)], table_sem.at[k * 2 + n])
-        for k, (src, dst) in enumerate([(ty_hbm, ty_ref), (tyk_hbm, tyk_ref)])
-        for n in range(2)
-    ]
+    pairs = [(cot_hbm, cot_ref), (tx_hbm, tx_ref), (state_hbm, state_ref)]
+    for src, dst in [(ty_hbm, ty_ref), (tyk_hbm, tyk_ref)]:
+        pairs += [(src, dst.at[pl.ds(0, half)]), (src, dst.at[pl.ds(half, half)])]
+    pairs += [(tz_hbm, tz_ref), (tzk_hbm, tzk_ref), (tzt_hbm, tzt_ref), (tzkt_hbm, tzkt_ref), (perm_hbm, perm_ref)]
+    pairs += [(back_hbm, back_ref), (w_in_hbm, w_in_t), (b_hbm, b_row), (w_out_hbm, w_out)]
+    loads = [pltpu.make_async_copy(src, dst, load_sem.at[n]) for n, (src, dst) in enumerate(pairs)]
     for load in loads:
         load.start()
+    lax.fori_loop(0, NDEV - 1, greet, 0, unroll=3)
 
     def copy(src, dst, number, where):
         return pltpu.make_async_remote_copy(
@@ -155,13 +155,15 @@
             return carry
 
         dst[pl.ds(me, 1)] = src[pl.ds(me, 1)]
-        lax.fori_loop(0, NDEV - 1, send, 0)
+        lax.fori_loop(0, NDEV - 1, send, 0, unroll=3)
 
     def whole(src, dst, number):
         rest = pl.ds(0, NDEV - 1)
         return copy(src.at[rest], dst.at[rest], number, peer(0)[1])
 
     for group in range(3):
+        for load in [loads[0:2], loads[2:3], []][group]:
+            load.wait()
 
         def one(mp, carry):
             for mh in range(3):
@@ -189,7 +191,7 @@
                     re, im = value[f]
                     top = jnp.concatenate([re, im], axis=1)
                     low = jnp.concatenate([im, -re], axis=1)
-                    row = pl.multiple_of(lax.rem((f * 3 + mh) % 8 + j, 8) * SLOT, 16)
+                    row = pl.multiple_of((((f * 3 + mh) % 8 + j) & 7) * SLOT, 16)
                     s_ref[pl.ds(row, SLOT), :] = jnp.concatenate([top, low], axis=0).astype(BF16)
             for first in range(0, ROW, 256):
                 width = min(256, ROW - first)
@@ -218,16 +220,15 @@
     lane = lax.broadcasted_iota(jnp.int32, (1, 128), 1).astype(BF16)
     lane = jnp.broadcast_to(lane, (128, 128))
 
+    for load in loads[3:]:
+        load.wait()
     perm = perm_ref[...]
     win[...] = dot(w_in_t[...], perm, TN).astype(BF16)
     wint[...] = dot(perm, w_in_t[...], TN).astype(BF16)
     woutt[...] = dot(w_out[...], perm, TN).astype(BF16)
     gin[...] = jnp.zeros_like(gin)
     gout[...] = jnp.zeros_like(gout)
-    for c in range(4):
-        l32[(c * 22 + 15) * 128 : (c * 22 + 16) * 128, :] = jnp.zeros((128, 128), F32)
-    for load in loads:
-        load.wait()
+    bias[...] = jnp.broadcast_to(b_row[...], (128, HID)).T
 
     BLOCKS = 27
 
@@ -299,8 +300,9 @@
         force = [rows_of(6, bz) for bz in bzs]
         features = boxes(velocity)
         adjoints = boxes(force)
-        pre = dot(win[...], features) + b_ref[...]
-        sigmoid = 1.0 / (1.0 + jnp.exp(-pre))
+        shift = bias[...]
+        pre = dot(win[...], features) + jnp.concatenate([shift, shift], axis=1)
+        sigmoid = 0.5 + 0.5 * jnp.tanh(0.5 * pre)
         hidden = (pre * sigmoid).astype(BF16)
         hidden_adj = FORCING * dot(woutt[...], adjoints)
         pre_adj = (hidden_adj * sigmoid * (1.0 + pre * (1.0 - sigmoid))).astype(BF16)
@@ -336,12 +338,14 @@
             parts.append(jnp.concatenate([va32[0, pl.ds(row, 64), :], va32[1, pl.ds(row, 64), :]], axis=1))
         return jnp.concatenate(parts, axis=0).astype(BF16)
 
+    def l32_row(r, block):
+        return (r * 22 + block) * 128
+
     def put(block, value, xx):
         for r in range(2):
             for mh in range(3):
                 for h in range(2):
-                    row = ((2 * r + h) * 22 + block(mh)) * 128 + xx
-                    l32[pl.ds(row, 32, stride=4), :] = value[
+                    l32[h, pl.ds(l32_row(r, block(mh)) + xx, 32, stride=4), :] = value[
                         r * 96 + mh * 32 : r * 96 + (mh + 1) * 32, h * 128 : (h + 1) * 128
                     ]
 
@@ -370,10 +374,16 @@
         put(extra(0), value, xx)
         return carry
 
+    for r in range(2):
+        for h in range(2):
+            row = l32_row(r, 15)
+            l32[h, row : row + 128, :] = jnp.zeros((128, 128), F32)
     lax.fori_loop(0, 4, forward_z, 0)
 
     def left_of(block, count):
-        parts = [l32[(c * 22 + block) * 128 : (c * 22 + block + count) * 128, :] for c in range(4)]
+        parts = [
+            l32[h, l32_row(r, block) : l32_row(r, block + count), :] for r in range(2) for h in range(2)
+        ]
         return jnp.concatenate(parts, axis=1).astype(BF16)
 
     for pp in range(8):
@@ -394,7 +404,11 @@
 
     whole(gsent, ggot, GRADS).wait_recv()
     total = lax.fori_loop(0, NDEV, lambda d, t: t + ggot[d].astype(F32), jnp.zeros((16, 256), F32), unroll=4)
-    grad_ref[...] = dot(total, back_ref[...], precision=lax.Precision.HIGHEST)
+    ordered = dot(total, back_ref[...], precision=lax.Precision.HIGHEST)
+    grad_in_ref[...] = ordered[0:8, 0:FEAT]
+    grad_out_ref[...] = ordered[8:16, 0:FEAT]
+    pick = (lax.broadcasted_iota(jnp.int32, (8, 256), 1) == FEAT).astype(F32)
+    grad_bias_ref[...] = dot(pick, total[0:8], NT, precision=lax.Precision.HIGHEST)[0:1]
 
     for g in range(FWD):
         whole(back.at[g], mine.at[g], GRADS + 1 + g).wait_recv()
@@ -413,7 +427,11 @@
                     flat[pl.ds((g * 3 + c) * NDEV * PART + mp * 4 + xx, NDEV, stride=PART), :] for xx in range(4)
                 ]
                 left = jnp.concatenate(rows, axis=0).astype(BF16)
-                o32[mp, (g * 3 + c) * 128 : (g * 3 + c + 1) * 128, :] = dot(left, tx_ref[...], TN)
+                out = dot(left, tx_ref[...], TN)
+                for r in range(2):
+                    for h in range(2):
+                        row = pl.multiple_of((mp * 2 + r) * FWD * ROW + (g * 3 + c) * 128, 8)
+                        o32[h, pl.ds(row, 128), :] = out[:, (2 * r + h) * 128 : (2 * r + h + 1) * 128]
             return carry
 
         lax.fori_loop(0, 4, along_x, 0)
@@ -426,10 +444,9 @@
             parts = []
             for f in range(5):
                 g, pp = divmod(f * 3 + mh, 8)
-                row = pl.multiple_of(g * ROW + lax.rem(pp + j, 8) * SLOT, 8)
-                re = o32[mp, pl.ds(row, WY), :]
-                im = o32[mp, pl.ds(row + WY, WY), :]
-                parts.append((re[:, :NG] - im[:, NG:], im[:, :NG] + re[:, NG:]))
+                row = pl.multiple_of(mp * 2 * FWD * ROW + g * ROW + ((pp + j) & 7) * SLOT, 8)
+                wave = lambda r, s: jnp.concatenate([o32[h, pl.ds(row + r * FWD * ROW + s * WY, WY), :] for h in range(2)], axis=1)
+                parts.append((wave(0, 0) - wave(1, 1), wave(0, 1) + wave(1, 0)))
             ax, az, ay, wy, wz = parts
             spec = [
                 ax,
@@ -449,58 +466,51 @@
         whole(back.at[g], mine.at[g], GRADS + 1 + g).wait_send()
 
 
+ANY = pl.BlockSpec(memory_space=pltpu.HBM)
 VMEM = pl.BlockSpec(memory_space=pltpu.VMEM)
-ANY = pl.BlockSpec(memory_space=pl.ANY)
 
 
 def shards(state, cotangent, w_in, b_in, w_out):
     t = {k: jnp.asarray(v) for k, v in make_tables().items()}
-    state = state.transpose(0, 1, 3, 2, 4)
-    cotangent = cotangent.transpose(0, 1, 3, 2, 4)
     sds = jax.ShapeDtypeStruct
-    grad, sums = pl.pallas_call(
+    operands = [state.transpose(0, 1, 3, 2, 4), cotangent.transpose(0, 1, 3, 2, 4)]
+    operands += [t[k] for k in ("tx", "tz", "tzk", "tzt", "tzkt", "perm", "back")]
+    operands += [w_in.T, b_in[None, :], w_out]
+    grad, grad_in, grad_out, grad_bias = pl.pallas_call(
         main_kernel,
-        out_shape=(sds((3, 2, WZ, WY, NG), F32), sds((16, 256), F32)),
-        in_specs=[VMEM] * 12 + [ANY] * 2,
-        out_specs=(VMEM, VMEM),
-        scratch_shapes=[
+        out_shape=(sds((3, 2, WZ, WY, NG), F32), sds((8, FEAT), F32), sds((8, FEAT), F32), sds((1, 8), F32)),
+        in_specs=[ANY] * 14,
+        out_specs=(VMEM,) * 4,
+        scratch_shapes=[pltpu.VMEM(o.shape, o.dtype) for o in operands]
+        + [
             pltpu.VMEM((ROW, 2 * NG), BF16),
             pltpu.VMEM((4 * 27 * 128, 128), F32),
             pltpu.VMEM((3, NDEV, 16, ROW), BF16),
             pltpu.VMEM((3, NDEV, 16, ROW), BF16),
             pltpu.VMEM((2, 144 * PITCH, 128), F32),
             pltpu.VMEM((2, 96 * PITCH, 128), F32),
-            pltpu.VMEM((4 * 22 * 128, 128), F32),
             pltpu.VMEM((8, 256, ROW), BF16),
             pltpu.VMEM((FWD, NDEV, 16, ROW), BF16),
             pltpu.VMEM((FWD, NDEV, 16, ROW), BF16),
             pltpu.VMEM((NDEV, 16, 256), BF16),
             pltpu.VMEM((NDEV, 16, 256), BF16),
-            pltpu.VMEM((4, FWD * ROW, 2 * NG), F32),
             pltpu.VMEM((4 * KY, 2 * NG), BF16),
             pltpu.VMEM((4 * KY, 2 * NG), BF16),
             pltpu.VMEM((HID, FEAT), BF16),
             pltpu.VMEM((FEAT, HID), BF16),
             pltpu.VMEM((HID, FEAT), BF16),
+            pltpu.VMEM((HID, 128), F32),
             pltpu.VMEM((HID, 256), F32),
             pltpu.VMEM((HID, 256), F32),
-            pltpu.SemaphoreType.DMA((4,)),
+            pltpu.SemaphoreType.DMA((16,)),
             pltpu.SemaphoreType.DMA((6,)),
             pltpu.SemaphoreType.DMA((6,)),
         ],
         compiler_params=pltpu.CompilerParams(
-            collective_id=0, has_side_effects=True, vmem_limit_bytes=64000 * 1024
+            collective_id=0, has_side_effects=True, vmem_limit_bytes=LIMIT
         ),
-    )(
-        state, cotangent, t["tx"], t["tz"], t["tzk"], t["tzt"], t["tzkt"], t["perm"], t["back"],
-        w_in.T, b_in[:, None], w_out, t["ty"], t["tyk"],
-    )
-    return (
-        grad.transpose(0, 1, 3, 2, 4),
-        sums[0:8, 0:FEAT],
-        sums[8:16, 0:FEAT].T,
-        sums[0:8, FEAT][None, :],
-    )
+    )(*[pltpu.with_memory_space_constraint(o, pltpu.HBM) for o in [*operands, t["ty"], t["tyk"]]])
+    return grad.transpose(0, 1, 3, 2, 4), grad_in, grad_out.T, grad_bias
 
 
 def solution(mesh):

time: 97 us -> 86.2 us (0.89)
  Pallas kernels: 89 us -> 82.5 us
  local copies, waits for them, and re-layouts: 7.1 us -> 2.92 us
    pallas_call x1, Pallas kernels: 89 us -> 82.5 us  [shards(): pl.pallas_call(main_kernel, out_shape=(sds((3, 2, WZ, WY, NG), F32), sds(...]
    broadcast_in_dim x1 -> x0, local copies, waits for them, and re-layouts: 1.54 us -> none  [shards(): b_in[:, None]]
    slice x1 -> x0, local copies, waits for them, and re-layouts: 1.38 us -> none  [shards(): sums[0:8, FEAT][None, :]]
    transpose x1 -> x0, local copies, waits for them, and re-layouts: 1.32 us -> none  [shards(): sums[8:16, 0:FEAT]]
    unnamed x1 -> x4, local copies, waits for them, and re-layouts: 2.87 us -> 2.92 us
where the time goes in v2:
time: 86.2 us; the launch traced here: 86.1 us
  Pallas kernels  82.5 us (96%)
  local copies, waits for them, and re-layouts  2.92 us (3%)
    pallas_call x1, Pallas kernels, shards(): pl.pallas_call(main_kernel, out_shape=(sds((3, 2, WZ, WY, NG), F32), sds(...  82.5 us
    unnamed x4, local copies, waits for them, and re-layouts  2.92 us

profile of v2, /device:TPU:1, one launch (start us, length us, event | category | flops | bytes accessed | tf_op | source)
XLA Modules:
  0.0 86.1 jit_solution(2169148831121745787)
XLA Ops:
  0.6 82.5 %shard_map.165 = (f32[3,2,12,24,256]{4,3,2,1,0:T(8,128)S(1)}, f32[8,192]{1,0:T(8,128)S(1)}, f32[8,192]{1,0:T(8,128)S(1)}, f32[1,8]{1,0:T(1,128)S(1)}) custom-call(f32[3,2,12,24,256]{4,3,2,1,0:T(8,128)} %bitcast.8, f32[3,2,12,24,256]{4,3,2,1,0:T(8,128)} %bitcast.9, bf16[256,512]{1,0:T(8,128)(2,1)} %constant.18.clone.tx_hbm, ...), custom_call_target="tpu_custom_call" | custom-call | tf_op jit(solution)/shard_map/pallas_call | solution.py:479
  83.2 1.2 %copy.22 = f32[3,2,24,12,256]{4,2,3,1,0:T(8,128)} copy(f32[3,2,24,12,256]{4,2,3,1,0:T(8,128)S(1)} %bitcast.6) | data formatting | bytes 3538944
  84.4 0.6 copy.23
  85.0 0.6 copy.24
  85.6 0.5 copy.25

commit v3 on v2

--- a/solution.py
+++ b/solution.py
@@ -25,6 +25,7 @@
 ROW = 8 * SLOT
 INV = 8
 FWD = 2
+SPARE = 208
 PITCH = 72
 
 
@@ -83,7 +84,8 @@
     return kx, ky, kz, retained, square, damping, weight
 
 
-LIMIT = 46 * 1024 * 1024
+LIMIT = 52 * 1024 * 1024
+LINES = FWD * ROW + 128
 PART = 24
 GRADS = INV * 3 // 8
 
@@ -105,13 +107,13 @@
     ty_hbm, tyk_hbm,
     out_ref, grad_in_ref, grad_out_ref, grad_bias_ref,
     state_ref, cot_ref, tx_ref, tz_ref, tzk_ref, tzt_ref, tzkt_ref, perm_ref, back_ref, w_in_t, b_row, w_out,
-    s_ref, flat, sent, got, v32, va32, o16, back, mine, gsent, ggot, ty_ref, tyk_ref,
-    win, wint, woutt, bias, gin, gout, load_sem, send_sem, recv_sem,
+    s_ref, flat, sent, got, v32, va32, o16, mine, gsent, ggot, ty_ref, tyk_ref,
+    win, wint, woutt, bias, gin, gout, hid_all, pre_all, feat_all, adj_all, ky_part, spare, load_sem, send_sem, recv_sem,
 ):
     j, l = lax.axis_index("px"), lax.axis_index("py")
     me = j * 8 + l
     x, core, z, y = j >> 1, j & 1, l >> 2, l & 3
-    l32, o32 = v32, va32
+    l32, o32, kz_part, back = flat, v32, state_ref, sent
 
     def peer(k):
         k = k + jnp.where(k >= 3, 1, 0)
@@ -173,7 +175,7 @@
                 value = {}
                 if any(f >= 3 for f in fields):
                     scale = weight * retained
-                    v = [[scale * state_ref[c, r, m] for r in range(2)] for c in range(3)]
+                    v = [[scale * state_ref[(c * 2 + r) * WZ + m] for r in range(2)] for c in range(3)]
                     value.update({3 + c: v[c] for c in range(3)})
                     value[6] = [-(kz * v[0][1] - kx * v[2][1]), kz * v[0][0] - kx * v[2][0]]
                     value[7] = [-(kx * v[1][1] - ky * v[0][1]), kx * v[1][0] - ky * v[0][0]]
@@ -228,6 +230,7 @@
     woutt[...] = dot(w_out[...], perm, TN).astype(BF16)
     gin[...] = jnp.zeros_like(gin)
     gout[...] = jnp.zeros_like(gout)
+    feat_all[FEAT:256, :] = jnp.ones((256 - FEAT, 4096), BF16)
     bias[...] = jnp.broadcast_to(b_row[...], (128, HID)).T
 
     BLOCKS = 27
@@ -276,133 +279,187 @@
 
         lax.fori_loop(0, 4, one, 0)
 
-    for group, fields in enumerate([[(6, 0), (7, 1)], [(8, 2), (0, 3), (1, 4)], [(2, 5), (3, INV), (4, 6), (5, 7)]]):
+    def boxes(fields):
+        def one(group, carry):
+            cols = pl.ds(pl.multiple_of(group * 256, 256), 256)
+            for slot, ref, c in fields:
+                rows = [pl.ds(slot * 16 * PITCH + group * 4 + b, 16, stride=PITCH) for b in range(4)]
+                planes = [[v32[h, r, :] for h in range(2)] for r in rows]
+                for dy in range(4):
+                    h, at = dy // 2, dy % 2 * 64
+                    value = jnp.concatenate([q[h][:, at : at + 64] for q in planes], axis=1)
+                    ref[dy * 48 + c * 16 : dy * 48 + (c + 1) * 16, cols] = value.astype(BF16)
+            return carry
+
+        lax.fori_loop(0, 16, one, 0, unroll=4 if len(fields) == 1 else 1)
+
+    for group, fields in enumerate([[(6, 0), (7, 1)], [(8, 2), (0, 3), (1, 4)], [(2, 5)]]):
         whole(sent.at[group], got.at[group], group).wait_recv()
         along_y(group)
         along_z(fields)
-
-    ones = jnp.ones((64, 256), BF16)
+        if group == 1:
+            boxes([(6, adj_all, 0), (7, adj_all, 1), (8, adj_all, 2), (0, feat_all, 0), (1, feat_all, 1)])
+    for group in range(3):
+        whole(sent.at[group], got.at[group], group).wait_send()
+
+    def put(first, value, xx):
+        for r in range(2):
+            for mh in range(3):
+                for h in range(2):
+                    part = value[r * 96 + mh * 32 : r * 96 + (mh + 1) * 32, h * 128 : (h + 1) * 128]
+                    if first < 12:
+                        va32[h, pl.ds((r * 12 + first + mh) * 128 + xx, 32, stride=4), :] = part
+                    else:
+                        l32[pl.ds(((2 * r + h) * 9 + first + mh - 12) * 128 + xx, 32, stride=4), :] = part
+
+    def plane(ref, c, xx, dz):
+        row = pl.multiple_of((c * 16 + xx * 4 + dz) * PITCH, 8)
+        return jnp.concatenate([ref[0, pl.ds(row, 64), :], ref[1, pl.ds(row, 64), :]], axis=1)
+
+    def vort_z(xx, carry):
+        parts = [[], [], []]
+        for dz in range(4):
+            vel = [plane(v32, c, xx, dz) for c in range(3)]
+            frc = [plane(v32, 6 + c, xx, dz) for c in range(3)]
+            for c, value in enumerate(cross(frc, vel)):
+                parts[c].append(value.astype(BF16))
+        wx, wy, wz = [jnp.concatenate(q, axis=0) for q in parts]
+        tzt = tzt_ref[...]
+        tzkt = tzkt_ref[...]
+        kz_part[pl.ds(xx * 16, 8)] = dot(tzkt, wy).reshape(8, WY, NG)
+        kz_part[pl.ds(xx * 16 + 8, 8)] = dot(tzkt, wx).reshape(8, WY, NG)
+        put(0, dot(tzt, wy), xx)
+        value = dot(tzt, wz)
+        put(3, value, xx)
+        put(6, value, xx)
+        put(9, -dot(tzt, wx), xx)
+        return carry
+
+    def back_y(block, pp, table):
+        first = (8 - pp) * SLOT
+        parts = []
+        for r in range(2):
+            for h in range(2):
+                if block < 12:
+                    parts.append(va32[h, (r * 12 + block) * 128 : (r * 12 + block + 1) * 128, :])
+                else:
+                    row = ((2 * r + h) * 9 + block - 12) * 128
+                    parts.append(l32[row : row + 128, :])
+        return dot(jnp.concatenate(parts, axis=1).astype(BF16), table[first : first + 2 * KY, :], NT)
+
+    def leave(g, used):
+        for to in range(8):
+            for v in range(3):
+                pick = lambda q: o16[(q - to) % 8 % used, :, v * 128 : (v + 1) * 128]
+                back[g, to * 8 : to * 8 + 8, :, v * 128 : (v + 1) * 128] = lane_select(lane, v, pick).reshape(8, 16, 128)
+        send_all(back.at[g], mine.at[g], GRADS + 1 + g)
+
+    lax.fori_loop(0, 4, vort_z, 0)
+    for pp in range(6):
+        o16[pp] = back_y(pp, pp, ty_ref).astype(BF16)
+    leave(0, 6)
+    for pp in range(6):
+        ky_part[pp] = back_y(6 + pp, pp, tyk_ref)
+    boxes([(2, feat_all, 2)])
+    along_z([(3, INV), (4, 6), (5, 7)])
 
     def rows_of(field, bz):
         rows = pl.ds(field * 16 * PITCH + bz, 48, stride=PITCH)
         return [v32[h, rows, :] for h in range(2)]
 
-    def boxes(planes):
-        parts = []
-        for dy in range(4):
-            h, at = dy // 2, dy % 2 * 64
-            parts.append(jnp.concatenate([p[h][:, at : at + 64] for p in planes], axis=1))
-        return jnp.concatenate(parts, axis=0).astype(BF16)
-
     def closure(group, carry):
         bzs = [group * 4 + b for b in range(4)]
-        velocity = [rows_of(0, bz) for bz in bzs]
-        force = [rows_of(6, bz) for bz in bzs]
-        features = boxes(velocity)
-        adjoints = boxes(force)
+        cols = pl.ds(pl.multiple_of(group * 256, 256), 256)
+        features = feat_all[0:FEAT, cols]
+        adjoints = adj_all[:, cols]
         shift = bias[...]
         pre = dot(win[...], features) + jnp.concatenate([shift, shift], axis=1)
         sigmoid = 0.5 + 0.5 * jnp.tanh(0.5 * pre)
-        hidden = (pre * sigmoid).astype(BF16)
+        hid_all[:, cols] = (pre * sigmoid).astype(BF16)
         hidden_adj = FORCING * dot(woutt[...], adjoints)
         pre_adj = (hidden_adj * sigmoid * (1.0 + pre * (1.0 - sigmoid))).astype(BF16)
-        gin[...] += dot(pre_adj, jnp.concatenate([features, ones], axis=0), NT)
-        gout[:, 0:FEAT] += dot(hidden, adjoints, NT)
+        pre_all[:, cols] = pre_adj
         feat_adj = dot(wint[...], pre_adj)
         for b, bz in enumerate(bzs):
-            spin = rows_of(3, bz)
+            spin, force = rows_of(3, bz), rows_of(6, bz)
             for h in range(2):
                 lanes = [feat_adj[dy * 48 : (dy + 1) * 48, b * 64 : (b + 1) * 64] for dy in (2 * h, 2 * h + 1)]
                 pick = lambda a: [a[c * 16 : (c + 1) * 16, :] for c in range(3)]
-                vel, vor, frc = pick(velocity[b][h]), pick(spin[h]), pick(force[b][h])
-                first = jnp.concatenate(cross(vor, frc), axis=0) + jnp.concatenate(lanes, axis=1)
-                second = jnp.concatenate(cross(frc, vel), axis=0)
-                va32[h, pl.ds(bz, 48, stride=PITCH), :] = first
-                va32[h, pl.ds(48 * PITCH + bz, 48, stride=PITCH), :] = second
-        return carry
-
-    lax.fori_loop(0, 16, closure, 0)
+                first = jnp.concatenate(cross(pick(spin[h]), pick(force[h])), axis=0)
+                va32[h, pl.ds(bz, 48, stride=PITCH), :] = first + jnp.concatenate(lanes, axis=1)
+        return carry
+
+    lax.fori_loop(0, 16, closure, 0, unroll=2)
+
+    def vel_z(xx, carry):
+        tzt = tzt_ref[...]
+        field = lambda c: jnp.concatenate([plane(va32, c, xx, dz).astype(BF16) for dz in range(4)], axis=0)
+        put(12, dot(tzt, field(0)) - kz_part[pl.ds(xx * 16, 8)].reshape(KY, NG), xx)
+        put(15, dot(tzt, field(2)), xx)
+        put(18, dot(tzt, field(1)) + kz_part[pl.ds(xx * 16 + 8, 8)].reshape(KY, NG), xx)
+        return carry
+
+    lax.fori_loop(0, 4, vel_z, 0)
+    for pp in range(8):
+        out = back_y(12 + pp, pp, ty_ref)
+        o16[pp] = (out + ky_part[pp] if pp < 6 else out).astype(BF16)
+    leave(1, 8)
+    ninth = back_y(20, 0, ty_ref)
+    for to in range(8):
+        piece = ninth[:, to * SLOT : (to + 1) * SLOT]
+        spare[to] = jnp.concatenate([jnp.zeros((128, SPARE - 128), F32), piece], axis=1)
+
+    def products(k, carry):
+        cols = pl.ds(pl.multiple_of(k * 1024, 1024), 1024)
+        gin[...] += dot(pre_all[:, cols], feat_all[:, cols], NT)
+        gout[:, 0:FEAT] += dot(hid_all[:, cols], adj_all[:, cols], NT)
+        return carry
+
+    lax.fori_loop(0, 4, products, 0)
+    own_lane = lax.broadcasted_iota(jnp.int32, (16, 128), 1) < SPARE - 128
 
     def slices(d, carry):
         rows = pl.ds(pl.multiple_of(d * 8, 8), 8)
-        gsent[d] = jnp.concatenate([gin[rows, :], FORCING * gout[rows, :]], axis=0).astype(BF16)
+        extra = spare[d >> 3, pl.ds(pl.multiple_of((d & 7) * 16, 16), 16), :]
+        lo = jnp.concatenate([gin[rows, 0:128], FORCING * gout[rows, 0:128]], axis=0)
+        hi = jnp.concatenate([gin[rows, 128:256], FORCING * gout[rows, 128:256]], axis=0)
+        gsent[d, :, 0:128] = lo.astype(BF16)
+        gsent[d, :, 128:256] = jnp.where(own_lane, hi, extra).astype(BF16)
         return carry
 
     lax.fori_loop(0, NDEV, slices, 0, unroll=4)
     send_all(gsent, ggot, GRADS)
 
-    def field_of(c, xx):
-        parts = []
-        for dz in range(4):
-            row = pl.multiple_of((c * 16 + xx * 4 + dz) * PITCH, 8)
-            parts.append(jnp.concatenate([va32[0, pl.ds(row, 64), :], va32[1, pl.ds(row, 64), :]], axis=1))
-        return jnp.concatenate(parts, axis=0).astype(BF16)
-
-    def l32_row(r, block):
-        return (r * 22 + block) * 128
-
-    def put(block, value, xx):
-        for r in range(2):
-            for mh in range(3):
-                for h in range(2):
-                    l32[h, pl.ds(l32_row(r, block(mh)) + xx, 32, stride=4), :] = value[
-                        r * 96 + mh * 32 : r * 96 + (mh + 1) * 32, h * 128 : (h + 1) * 128
-                    ]
-
-    def direct(f):
-        def block(mh):
-            g, pp = divmod(f * 3 + mh, 8)
-            return pp * 2 + g
-
-        return block
-
-    def extra(f):
-        return lambda mh: 16 + f * 3 + mh
-
-    def forward_z(xx, carry):
-        vort = field_of(4, xx)
-        tzt = tzt_ref[...]
-        tzkt = tzkt_ref[...]
-        put(direct(0), dot(tzt, field_of(0, xx)) - dot(tzkt, vort), xx)
-        put(direct(3), dot(tzt, vort), xx)
-        vort = field_of(3, xx)
-        put(direct(2), dot(tzt, field_of(1, xx)) + dot(tzkt, vort), xx)
-        put(extra(1), -dot(tzt, vort), xx)
-        put(direct(1), dot(tzt, field_of(2, xx)), xx)
-        value = dot(tzt, field_of(5, xx))
-        put(direct(4), value, xx)
-        put(extra(0), value, xx)
-        return carry
-
-    for r in range(2):
-        for h in range(2):
-            row = l32_row(r, 15)
-            l32[h, row : row + 128, :] = jnp.zeros((128, 128), F32)
-    lax.fori_loop(0, 4, forward_z, 0)
-
-    def left_of(block, count):
-        parts = [
-            l32[h, l32_row(r, block) : l32_row(r, block + count), :] for r in range(2) for h in range(2)
-        ]
-        return jnp.concatenate(parts, axis=1).astype(BF16)
-
-    for pp in range(8):
-        first = (8 - pp) * SLOT
-        out = dot(left_of(pp * 2, 2), ty_ref[first : first + 2 * KY, :], NT)
-        if pp < 6:
-            more = dot(left_of(16 + pp, 1), tyk_ref[first : first + 2 * KY, :], NT)
-            o16[pp, 0:128, :] = (out[0:128] + more).astype(BF16)
-            o16[pp, 128:256, :] = out[128:256].astype(BF16)
-        else:
-            o16[pp] = out.astype(BF16)
+    def arrive(ref, chunk, lanes):
+        def unpack(d, carry):
+            row = pl.multiple_of((chunk * NDEV + d) * PART, 8)
+            flat[pl.ds(row, 16), :] = ref[d, :, lanes : lanes + 128].astype(F32)
+            return carry
+
+        lax.fori_loop(0, NDEV, unpack, 0, unroll=8)
+
+    def along_x(chunks):
+        def one(mp, carry):
+            for c in chunks:
+                rows = [flat[pl.ds(c * NDEV * PART + mp * 4 + xx, NDEV, stride=PART), :] for xx in range(4)]
+                out = dot(jnp.concatenate(rows, axis=0).astype(BF16), tx_ref[...], TN)
+                for r in range(2):
+                    for h in range(2):
+                        row = pl.multiple_of((mp * 2 + r) * LINES + c * 128, 8)
+                        o32[h, pl.ds(row, 128), :] = out[:, (2 * r + h) * 128 : (2 * r + h + 1) * 128]
+            return carry
+
+        lax.fori_loop(0, 4, one, 0)
+
     for g in range(FWD):
-        for to in range(8):
-            for v in range(3):
-                pick = lambda q: o16[(q - to) % 8, g * 128 : (g + 1) * 128, v * 128 : (v + 1) * 128]
-                back[g, to * 8 : to * 8 + 8, :, v * 128 : (v + 1) * 128] = lane_select(lane, v, pick).reshape(8, 16, 128)
-        send_all(back.at[g], mine.at[g], GRADS + 1 + g)
-
+        whole(back.at[g], mine.at[g], GRADS + 1 + g).wait_recv()
+        for c in range(3):
+            arrive(mine.at[g], g * 3 + c, c * 128)
+        along_x(range(g * 3, g * 3 + 3))
     whole(gsent, ggot, GRADS).wait_recv()
+    arrive(ggot, 6, 128)
+    along_x([6])
+
     total = lax.fori_loop(0, NDEV, lambda d, t: t + ggot[d].astype(F32), jnp.zeros((16, 256), F32), unroll=4)
     ordered = dot(total, back_ref[...], precision=lax.Precision.HIGHEST)
     grad_in_ref[...] = ordered[0:8, 0:FEAT]
@@ -410,44 +467,18 @@
     pick = (lax.broadcasted_iota(jnp.int32, (8, 256), 1) == FEAT).astype(F32)
     grad_bias_ref[...] = dot(pick, total[0:8], NT, precision=lax.Precision.HIGHEST)[0:1]
 
-    for g in range(FWD):
-        whole(back.at[g], mine.at[g], GRADS + 1 + g).wait_recv()
-
-        def unpack(d, carry):
-            for c in range(3):
-                row = pl.multiple_of(((g * 3 + c) * NDEV + d) * PART, 8)
-                flat[pl.ds(row, 16), :] = mine[g, d, :, c * 128 : (c + 1) * 128].astype(F32)
-            return carry
-
-        lax.fori_loop(0, NDEV, unpack, 0, unroll=4)
-
-        def along_x(mp, carry):
-            for c in range(3):
-                rows = [
-                    flat[pl.ds((g * 3 + c) * NDEV * PART + mp * 4 + xx, NDEV, stride=PART), :] for xx in range(4)
-                ]
-                left = jnp.concatenate(rows, axis=0).astype(BF16)
-                out = dot(left, tx_ref[...], TN)
-                for r in range(2):
-                    for h in range(2):
-                        row = pl.multiple_of((mp * 2 + r) * FWD * ROW + (g * 3 + c) * 128, 8)
-                        o32[h, pl.ds(row, 128), :] = out[:, (2 * r + h) * 128 : (2 * r + h + 1) * 128]
-            return carry
-
-        lax.fori_loop(0, 4, along_x, 0)
-
     def finish(mp, carry):
         for mh in range(3):
             m = mh * 4 + mp
             kx, ky, kz, retained, square, damping, weight = waves_of(m, j, l)
             scale = weight * retained
             parts = []
-            for f in range(5):
-                g, pp = divmod(f * 3 + mh, 8)
-                row = pl.multiple_of(mp * 2 * FWD * ROW + g * ROW + ((pp + j) & 7) * SLOT, 8)
-                wave = lambda r, s: jnp.concatenate([o32[h, pl.ds(row + r * FWD * ROW + s * WY, WY), :] for h in range(2)], axis=1)
+            for g, piece in [(0, mh), (0, 3 + mh), (1, mh), (1, 3 + mh), (1, 6 + mh)]:
+                place = g * ROW + ((piece + j) & 7) * SLOT if piece < 8 else FWD * ROW + SPARE - 128
+                row = pl.multiple_of(mp * 2 * LINES + place, 8)
+                wave = lambda r, s: jnp.concatenate([o32[h, pl.ds(row + r * LINES + s * WY, WY), :] for h in range(2)], axis=1)
                 parts.append((wave(0, 0) - wave(1, 1), wave(0, 1) + wave(1, 0)))
-            ax, az, ay, wy, wz = parts
+            wy, wz, ax, az, ay = parts
             spec = [
                 ax,
                 (ay[0] + kx * wz[1], ay[1] - kx * wz[0]),
@@ -459,8 +490,6 @@
         return carry
 
     lax.fori_loop(0, 4, finish, 0)
-    for group in range(3):
-        whole(sent.at[group], got.at[group], group).wait_send()
     whole(gsent, ggot, GRADS).wait_send()
     for g in range(FWD):
         whole(back.at[g], mine.at[g], GRADS + 1 + g).wait_send()
@@ -473,7 +502,7 @@
 def shards(state, cotangent, w_in, b_in, w_out):
     t = {k: jnp.asarray(v) for k, v in make_tables().items()}
     sds = jax.ShapeDtypeStruct
-    operands = [state.transpose(0, 1, 3, 2, 4), cotangent.transpose(0, 1, 3, 2, 4)]
+    operands = [state.transpose(0, 1, 3, 2, 4).reshape(6 * WZ, WY, NG), cotangent.transpose(0, 1, 3, 2, 4)]
     operands += [t[k] for k in ("tx", "tz", "tzk", "tzt", "tzkt", "perm", "back")]
     operands += [w_in.T, b_in[None, :], w_out]
     grad, grad_in, grad_out, grad_bias = pl.pallas_call(
@@ -488,9 +517,8 @@
             pltpu.VMEM((3, NDEV, 16, ROW), BF16),
             pltpu.VMEM((3, NDEV, 16, ROW), BF16),
             pltpu.VMEM((2, 144 * PITCH, 128), F32),
-            pltpu.VMEM((2, 96 * PITCH, 128), F32),
-            pltpu.VMEM((8, 256, ROW), BF16),
-            pltpu.VMEM((FWD, NDEV, 16, ROW), BF16),
+            pltpu.VMEM((2, 48 * PITCH, 128), F32),
+            pltpu.VMEM((8, 128, ROW), BF16),
             pltpu.VMEM((FWD, NDEV, 16, ROW), BF16),
             pltpu.VMEM((NDEV, 16, 256), BF16),
             pltpu.VMEM((NDEV, 16, 256), BF16),
@@ -502,6 +530,12 @@
             pltpu.VMEM((HID, 128), F32),
             pltpu.VMEM((HID, 256), F32),
             pltpu.VMEM((HID, 256), F32),
+            pltpu.VMEM((HID, 4096), BF16),
+            pltpu.VMEM((HID, 4096), BF16),
+            pltpu.VMEM((256, 4096), BF16),
+            pltpu.VMEM((FEAT, 4096), BF16),
+            pltpu.VMEM((6, 128, ROW), F32),
+            pltpu.VMEM((8, 128, 128), F32),
             pltpu.SemaphoreType.DMA((16,)),
             pltpu.SemaphoreType.DMA((6,)),
             pltpu.SemaphoreType.DMA((6,)),

time: 86.2 us -> 80.8 us (0.937)
  Pallas kernels: 82.5 us -> 77.2 us
    pallas_call x1, Pallas kernels: 82.5 us -> 77.2 us  [shards(): pl.pallas_call(main_kernel, out_shape=(sds((3, 2, WZ, WY, NG), F32), sds(...]
where the time goes in v3:
time: 80.8 us; the launch traced here: 80.7 us
  Pallas kernels  77.2 us (96%)
  local copies, waits for them, and re-layouts  2.92 us (4%)
    pallas_call x1, Pallas kernels, shards(): pl.pallas_call(main_kernel, out_shape=(sds((3, 2, WZ, WY, NG), F32), sds(...  77.2 us
    unnamed x4, local copies, waits for them, and re-layouts  2.92 us

profile of v3, /device:TPU:1, one launch (start us, length us, event | category | flops | bytes accessed | tf_op | source)
XLA Modules:
  0.0 80.7 jit_solution(7776019459029170208)
XLA Ops:
  0.6 77.2 %shard_map.165 = (f32[3,2,12,24,256]{4,3,2,1,0:T(8,128)S(1)}, f32[8,192]{1,0:T(8,128)S(1)}, f32[8,192]{1,0:T(8,128)S(1)}, f32[1,8]{1,0:T(1,128)S(1)}) custom-call(f32[72,24,256]{2,1,0:T(8,128)} %bitcast.10, f32[3,2,12,24,256]{4,3,2,1,0:T(8,128)} %bitcast.11, bf16[256,512]{1,0:T(8,128)(2,1)} %constant.18.clone.tx_hbm, ...), custom_call_target="tpu_custom_call" | custom-call | tf_op jit(solution)/shard_map/pallas_call | solution.py:508
  77.8 1.2 %copy.22 = f32[3,2,24,12,256]{4,2,3,1,0:T(8,128)} copy(f32[3,2,24,12,256]{4,2,3,1,0:T(8,128)S(1)} %bitcast.8) | data formatting | bytes 3538944
  79.0 0.6 copy.23
  79.6 0.6 copy.24
  80.2 0.5 copy.25

commit v4 on v3

--- a/solution.py
+++ b/solution.py
@@ -24,6 +24,8 @@
 SLOT = 48
 ROW = 8 * SLOT
 INV = 8
+FEW, LAST = 3, 2
+ORDER = (0, 1, FEW, LAST)
 FWD = 2
 SPARE = 208
 PITCH = 72
@@ -87,7 +89,14 @@
 LIMIT = 52 * 1024 * 1024
 LINES = FWD * ROW + 128
 PART = 24
-GRADS = INV * 3 // 8
+GRADS = 4
+
+
+def place(f, mh):
+    if f >= 6:
+        return LAST, f * 3 + mh - 18
+    g, pp = divmod(f * 3 + mh, 8)
+    return (FEW if g == 2 else g), pp
 
 
 def lane_select(lane, v, pick):
@@ -107,7 +116,7 @@
     ty_hbm, tyk_hbm,
     out_ref, grad_in_ref, grad_out_ref, grad_bias_ref,
     state_ref, cot_ref, tx_ref, tz_ref, tzk_ref, tzt_ref, tzkt_ref, perm_ref, back_ref, w_in_t, b_row, w_out,
-    s_ref, flat, sent, got, v32, va32, o16, mine, gsent, ggot, ty_ref, tyk_ref,
+    s_ref, flat, sent, got, sent_few, got_few, v32, va32, o16, mine, gsent, ggot, ty_ref, tyk_ref,
     win, wint, woutt, bias, gin, gout, hid_all, pre_all, feat_all, adj_all, ky_part, spare, load_sem, send_sem, recv_sem,
 ):
     j, l = lax.axis_index("px"), lax.axis_index("py")
@@ -163,13 +172,17 @@
         rest = pl.ds(0, NDEV - 1)
         return copy(src.at[rest], dst.at[rest], number, peer(0)[1])
 
-    for group in range(3):
-        for load in [loads[0:2], loads[2:3], []][group]:
+    ways = [(sent.at[g], got.at[g]) for g in range(3)] + [(sent_few, got_few)]
+    for group in ORDER:
+        for load in [loads[0:2], loads[2:3], [], []][group]:
             load.wait()
+        lanes = 128 if group == FEW else ROW
 
         def one(mp, carry):
             for mh in range(3):
-                fields = [f for f in range(INV) if (f * 3 + mh) // 8 == group]
+                fields = [f for f in range(INV) if place(f, mh)[0] == group]
+                if not fields:
+                    continue
                 m = mh * 4 + mp
                 kx, ky, kz, retained, square, damping, weight = waves_of(m, j, l)
                 value = {}
@@ -193,10 +206,11 @@
                     re, im = value[f]
                     top = jnp.concatenate([re, im], axis=1)
                     low = jnp.concatenate([im, -re], axis=1)
-                    row = pl.multiple_of((((f * 3 + mh) % 8 + j) & 7) * SLOT, 16)
+                    pp = place(f, mh)[1]
+                    row = pp * SLOT if group == FEW else pl.multiple_of(((pp + j) & 7) * SLOT, 16)
                     s_ref[pl.ds(row, SLOT), :] = jnp.concatenate([top, low], axis=0).astype(BF16)
-            for first in range(0, ROW, 256):
-                width = min(256, ROW - first)
+            for first in range(0, lanes, 256):
+                width = min(256, lanes - first)
                 out = dot(tx_ref[...], s_ref[first : first + width, :], NT)
                 for c in range(width // 128):
                     for xx in range(4):
@@ -209,15 +223,15 @@
         lax.fori_loop(0, 4, one, 0)
 
         def pack(d, carry):
-            for c in range(3):
+            for c in range(lanes // 128):
                 row = pl.multiple_of(c * NDEV * PART + d * PART, 8)
-                sent[group, d, :, c * 128 : (c + 1) * 128] = flat[pl.ds(row, 16), :].astype(BF16)
+                ways[group][0][d, :, c * 128 : (c + 1) * 128] = flat[pl.ds(row, 16), :].astype(BF16)
             return carry
 
         lax.fori_loop(0, NDEV, pack, 0, unroll=4)
         if group == 0:
             pl.semaphore_wait(barrier, NDEV - 1)
-        send_all(sent.at[group], got.at[group], group)
+        send_all(*ways[group], group)
 
     lane = lax.broadcasted_iota(jnp.int32, (1, 128), 1).astype(BF16)
     lane = jnp.broadcast_to(lane, (128, 128))
@@ -235,31 +249,44 @@
 
     BLOCKS = 27
 
+    def block_of(f, mh):
+        g, pp = place(f, mh)
+        return 24 + mh if f == INV else {0: 0, 1: 8, FEW: 16, LAST: 18}[g] + pp
+
     def along_y(group):
-        for pp in range(8):
-            first = (8 - pp) * SLOT
-            parts = []
-            for v in range(3):
-                pick = lambda q: got[group, (q - pp) % 8 * 8 : (q - pp) % 8 * 8 + 8, :, v * 128 : (v + 1) * 128].reshape(128, 128)
-                parts.append(lane_select(lane, v, pick))
-            left = jnp.concatenate(parts, axis=1)
-            todo = [(pp * 3 + group, dot(left, ty_ref[first : first + 2 * KY, :]))]
-            f, mh = divmod(group * 8 + pp, 3)
-            if f == 5:
-                todo.append((24 + mh, -dot(left, tyk_ref[first : first + 2 * KY, :])))
-            for block, out in todo:
-                for c in range(4):
-                    row = (c * BLOCKS + block) * 128
-                    flat[row : row + 128, :] = out[:, c * 128 : (c + 1) * 128]
+        for f in range(INV):
+            for mh in range(3):
+                g, pp = place(f, mh)
+                if g != group:
+                    continue
+                first = (8 - pp) * SLOT
+                parts = []
+                if group == FEW:
+                    first = 0
+                    for n in range(8):
+                        rows = got_few[n * 8 : n * 8 + 8].reshape(128, 128).astype(F32)
+                        parts.append(rows[:, pp * SLOT : (pp + 1) * SLOT])
+                else:
+                    for v in range(3):
+                        pick = lambda q: got[
+                            group, (q - pp) % 8 * 8 : (q - pp) % 8 * 8 + 8, :, v * 128 : (v + 1) * 128
+                        ].reshape(128, 128)
+                        parts.append(lane_select(lane, v, pick))
+                left = jnp.concatenate(parts, axis=1).astype(BF16)
+                todo = [(block_of(f, mh), dot(left, ty_ref[first : first + 2 * KY, :]))]
+                if f == 5:
+                    todo.append((24 + mh, -dot(left, tyk_ref[first : first + 2 * KY, :])))
+                for block, out in todo:
+                    for c in range(4):
+                        row = (c * BLOCKS + block) * 128
+                        flat[row : row + 128, :] = out[:, c * 128 : (c + 1) * 128]
 
     def columns(f, xx):
         parts = []
         for t in range(2):
             for mh in range(3):
-                g, pp = divmod(f * 3 + mh, 8)
-                block = 24 + mh if f == INV else pp * 3 + g
                 lanes = [
-                    flat[pl.ds(((2 * t + h) * BLOCKS + block) * 128 + xx, 32, stride=4), :] for h in range(2)
+                    flat[pl.ds(((2 * t + h) * BLOCKS + block_of(f, mh)) * 128 + xx, 32, stride=4), :] for h in range(2)
                 ]
                 parts.append(jnp.concatenate(lanes, axis=1))
         return jnp.concatenate(parts, axis=0).astype(BF16)
@@ -293,14 +320,14 @@
 
         lax.fori_loop(0, 16, one, 0, unroll=4 if len(fields) == 1 else 1)
 
-    for group, fields in enumerate([[(6, 0), (7, 1)], [(8, 2), (0, 3), (1, 4)], [(2, 5)]]):
-        whole(sent.at[group], got.at[group], group).wait_recv()
+    for group, fields in [(0, [(6, 0), (7, 1)]), (1, [(8, 2), (0, 3), (1, 4)]), (FEW, [(2, 5)])]:
+        whole(*ways[group], group).wait_recv()
         along_y(group)
         along_z(fields)
         if group == 1:
             boxes([(6, adj_all, 0), (7, adj_all, 1), (8, adj_all, 2), (0, feat_all, 0), (1, feat_all, 1)])
-    for group in range(3):
-        whole(sent.at[group], got.at[group], group).wait_send()
+    for group in (0, 1, FEW):
+        whole(*ways[group], group).wait_send()
 
     def put(first, value, xx):
         for r in range(2):
@@ -361,11 +388,6 @@
     for pp in range(6):
         ky_part[pp] = back_y(6 + pp, pp, tyk_ref)
     boxes([(2, feat_all, 2)])
-    along_z([(3, INV), (4, 6), (5, 7)])
-
-    def rows_of(field, bz):
-        rows = pl.ds(field * 16 * PITCH + bz, 48, stride=PITCH)
-        return [v32[h, rows, :] for h in range(2)]
 
     def closure(group, carry):
         bzs = [group * 4 + b for b in range(4)]
@@ -381,19 +403,26 @@
         pre_all[:, cols] = pre_adj
         feat_adj = dot(wint[...], pre_adj)
         for b, bz in enumerate(bzs):
-            spin, force = rows_of(3, bz), rows_of(6, bz)
             for h in range(2):
                 lanes = [feat_adj[dy * 48 : (dy + 1) * 48, b * 64 : (b + 1) * 64] for dy in (2 * h, 2 * h + 1)]
-                pick = lambda a: [a[c * 16 : (c + 1) * 16, :] for c in range(3)]
-                first = jnp.concatenate(cross(pick(spin[h]), pick(force[h])), axis=0)
-                va32[h, pl.ds(bz, 48, stride=PITCH), :] = first + jnp.concatenate(lanes, axis=1)
+                va32[h, pl.ds(bz, 48, stride=PITCH), :] = jnp.concatenate(lanes, axis=1)
         return carry
 
     lax.fori_loop(0, 16, closure, 0, unroll=2)
+
+    whole(*ways[LAST], LAST).wait_recv()
+    along_y(LAST)
+    along_z([(3, INV), (4, 6), (5, 7)])
 
     def vel_z(xx, carry):
         tzt = tzt_ref[...]
-        field = lambda c: jnp.concatenate([plane(va32, c, xx, dz).astype(BF16) for dz in range(4)], axis=0)
+        parts = [[], [], []]
+        for dz in range(4):
+            spin = [plane(v32, 3 + c, xx, dz) for c in range(3)]
+            frc = [plane(v32, 6 + c, xx, dz) for c in range(3)]
+            for c, value in enumerate(cross(spin, frc)):
+                parts[c].append((value + plane(va32, c, xx, dz)).astype(BF16))
+        field = lambda c: jnp.concatenate(parts[c], axis=0)
         put(12, dot(tzt, field(0)) - kz_part[pl.ds(xx * 16, 8)].reshape(KY, NG), xx)
         put(15, dot(tzt, field(2)), xx)
         put(18, dot(tzt, field(1)) + kz_part[pl.ds(xx * 16 + 8, 8)].reshape(KY, NG), xx)
@@ -490,6 +519,7 @@
         return carry
 
     lax.fori_loop(0, 4, finish, 0)
+    whole(*ways[LAST], LAST).wait_send()
     whole(gsent, ggot, GRADS).wait_send()
     for g in range(FWD):
         whole(back.at[g], mine.at[g], GRADS + 1 + g).wait_send()
@@ -516,6 +546,8 @@
             pltpu.VMEM((4 * 27 * 128, 128), F32),
             pltpu.VMEM((3, NDEV, 16, ROW), BF16),
             pltpu.VMEM((3, NDEV, 16, ROW), BF16),
+            pltpu.VMEM((NDEV, 16, 128), BF16),
+            pltpu.VMEM((NDEV, 16, 128), BF16),
             pltpu.VMEM((2, 144 * PITCH, 128), F32),
             pltpu.VMEM((2, 48 * PITCH, 128), F32),
             pltpu.VMEM((8, 128, ROW), BF16),
@@ -537,8 +569,8 @@
             pltpu.VMEM((6, 128, ROW), F32),
             pltpu.VMEM((8, 128, 128), F32),
             pltpu.SemaphoreType.DMA((16,)),
-            pltpu.SemaphoreType.DMA((6,)),
-            pltpu.SemaphoreType.DMA((6,)),
+            pltpu.SemaphoreType.DMA((7,)),
+            pltpu.SemaphoreType.DMA((7,)),
         ],
         compiler_params=pltpu.CompilerParams(
             collective_id=0, has_side_effects=True, vmem_limit_bytes=LIMIT

time: 80.8 us -> 76.7 us (0.949)
  Pallas kernels: 77.2 us -> 73 us
    pallas_call x1, Pallas kernels: 77.2 us -> 73 us  [shards(): pl.pallas_call(main_kernel, out_shape=(sds((3, 2, WZ, WY, NG), F32), sds(...]
where the time goes in v4:
time: 76.7 us; the launch traced here: 76.6 us
  Pallas kernels  73 us (95%)
  local copies, waits for them, and re-layouts  2.92 us (4%)
    pallas_call x1, Pallas kernels, shards(): pl.pallas_call(main_kernel, out_shape=(sds((3, 2, WZ, WY, NG), F32), sds(...  73 us
    unnamed x4, local copies, waits for them, and re-layouts  2.92 us

profile of v4, /device:TPU:1, one launch (start us, length us, event | category | flops | bytes accessed | tf_op | source)
XLA Modules:
  0.0 76.6 jit_solution(10461284413522832062)
XLA Ops:
  0.6 73.0 %shard_map.165 = (f32[3,2,12,24,256]{4,3,2,1,0:T(8,128)S(1)}, f32[8,192]{1,0:T(8,128)S(1)}, f32[8,192]{1,0:T(8,128)S(1)}, f32[1,8]{1,0:T(1,128)S(1)}) custom-call(f32[72,24,256]{2,1,0:T(8,128)} %bitcast.10, f32[3,2,12,24,256]{4,3,2,1,0:T(8,128)} %bitcast.11, bf16[256,512]{1,0:T(8,128)(2,1)} %constant.18.clone.tx_hbm, ...), custom_call_target="tpu_custom_call" | custom-call | tf_op jit(solution)/shard_map/pallas_call | solution.py:538
  73.7 1.2 %copy.22 = f32[3,2,24,12,256]{4,2,3,1,0:T(8,128)} copy(f32[3,2,24,12,256]{4,2,3,1,0:T(8,128)S(1)} %bitcast.8) | data formatting | bytes 3538944
  74.9 0.6 copy.23
  75.5 0.6 copy.24
  76.1 0.5 copy.25

commit v5 on v4

--- a/solution.py
+++ b/solution.py
@@ -304,7 +304,7 @@
                         v32[h, pl.ds(row, 64), :] = out[dz * 64 : (dz + 1) * 64, h * 128 : (h + 1) * 128]
             return carry
 
-        lax.fori_loop(0, 4, one, 0)
+        lax.fori_loop(0, 4, one, 0, unroll=4 if len(fields) == 1 else 2)
 
     def boxes(fields):
         def one(group, carry):
@@ -318,14 +318,16 @@
                     ref[dy * 48 + c * 16 : dy * 48 + (c + 1) * 16, cols] = value.astype(BF16)
             return carry
 
-        lax.fori_loop(0, 16, one, 0, unroll=4 if len(fields) == 1 else 1)
+        lax.fori_loop(0, 16, one, 0, unroll=4 if len(fields) == 1 else 2)
 
     for group, fields in [(0, [(6, 0), (7, 1)]), (1, [(8, 2), (0, 3), (1, 4)]), (FEW, [(2, 5)])]:
         whole(*ways[group], group).wait_recv()
         along_y(group)
         along_z(fields)
+        if group == 0:
+            boxes([(6, adj_all, 0), (7, adj_all, 1)])
         if group == 1:
-            boxes([(6, adj_all, 0), (7, adj_all, 1), (8, adj_all, 2), (0, feat_all, 0), (1, feat_all, 1)])
+            boxes([(8, adj_all, 2), (0, feat_all, 0), (1, feat_all, 1)])
     for group in (0, 1, FEW):
         whole(*ways[group], group).wait_send()
 
@@ -381,7 +383,7 @@
                 back[g, to * 8 : to * 8 + 8, :, v * 128 : (v + 1) * 128] = lane_select(lane, v, pick).reshape(8, 16, 128)
         send_all(back.at[g], mine.at[g], GRADS + 1 + g)
 
-    lax.fori_loop(0, 4, vort_z, 0)
+    lax.fori_loop(0, 4, vort_z, 0, unroll=2)
     for pp in range(6):
         o16[pp] = back_y(pp, pp, ty_ref).astype(BF16)
     leave(0, 6)
@@ -428,7 +430,7 @@
         put(18, dot(tzt, field(1)) + kz_part[pl.ds(xx * 16 + 8, 8)].reshape(KY, NG), xx)
         return carry
 
-    lax.fori_loop(0, 4, vel_z, 0)
+    lax.fori_loop(0, 4, vel_z, 0, unroll=2)
     for pp in range(8):
         out = back_y(12 + pp, pp, ty_ref)
         o16[pp] = (out + ky_part[pp] if pp < 6 else out).astype(BF16)
@@ -480,14 +482,46 @@
 
         lax.fori_loop(0, 4, one, 0)
 
+    def finish(late):
+        def one(mp, carry):
+            for mh in range(2 if late else 0, 3):
+                m = mh * 4 + mp
+                kx, ky, kz, retained, square, damping, weight = waves_of(m, j, l)
+                scale = weight * retained
+
+                def part(g, piece):
+                    at = g * ROW + ((piece + j) & 7) * SLOT if piece < 8 else FWD * ROW + SPARE - 128
+                    row = pl.multiple_of(mp * 2 * LINES + at, 8)
+                    wave = lambda r, s: jnp.concatenate(
+                        [o32[h, pl.ds(row + r * LINES + s * WY, WY), :] for h in range(2)], axis=1
+                    )
+                    return wave(0, 0) - wave(1, 1), wave(0, 1) + wave(1, 0)
+
+                spec = {}
+                if not late:
+                    az, wy = part(1, 3 + mh), part(0, mh)
+                    spec[0] = part(1, mh)
+                    spec[2] = (az[0] - kx * wy[1], az[1] + kx * wy[0])
+                if late or mh < 2:
+                    ay, wz = part(1, 6 + mh), part(0, 3 + mh)
+                    spec[1] = (ay[0] + kx * wz[1], ay[1] - kx * wz[0])
+                for c, value in spec.items():
+                    for r in range(2):
+                        out_ref[c, r, m] = damping * cot_ref[c, r, m] + scale * value[r]
+            return carry
+
+        lax.fori_loop(0, 4, one, 0)
+
     for g in range(FWD):
         whole(back.at[g], mine.at[g], GRADS + 1 + g).wait_recv()
         for c in range(3):
             arrive(mine.at[g], g * 3 + c, c * 128)
         along_x(range(g * 3, g * 3 + 3))
+    finish(False)
     whole(gsent, ggot, GRADS).wait_recv()
     arrive(ggot, 6, 128)
     along_x([6])
+    finish(True)
 
     total = lax.fori_loop(0, NDEV, lambda d, t: t + ggot[d].astype(F32), jnp.zeros((16, 256), F32), unroll=4)
     ordered = dot(total, back_ref[...], precision=lax.Precision.HIGHEST)
@@ -496,33 +530,19 @@
     pick = (lax.broadcasted_iota(jnp.int32, (8, 256), 1) == FEAT).astype(F32)
     grad_bias_ref[...] = dot(pick, total[0:8], NT, precision=lax.Precision.HIGHEST)[0:1]
 
-    def finish(mp, carry):
-        for mh in range(3):
-            m = mh * 4 + mp
-            kx, ky, kz, retained, square, damping, weight = waves_of(m, j, l)
-            scale = weight * retained
-            parts = []
-            for g, piece in [(0, mh), (0, 3 + mh), (1, mh), (1, 3 + mh), (1, 6 + mh)]:
-                place = g * ROW + ((piece + j) & 7) * SLOT if piece < 8 else FWD * ROW + SPARE - 128
-                row = pl.multiple_of(mp * 2 * LINES + place, 8)
-                wave = lambda r, s: jnp.concatenate([o32[h, pl.ds(row + r * LINES + s * WY, WY), :] for h in range(2)], axis=1)
-                parts.append((wave(0, 0) - wave(1, 1), wave(0, 1) + wave(1, 0)))
-            wy, wz, ax, az, ay = parts
-            spec = [
-                ax,
-                (ay[0] + kx * wz[1], ay[1] - kx * wz[0]),
-                (az[0] - kx * wy[1], az[1] + kx * wy[0]),
-            ]
-            for c in range(3):
-                for r in range(2):
-                    out_ref[c, r, m] = damping * cot_ref[c, r, m] + scale * spec[c][r]
-        return carry
-
-    lax.fori_loop(0, 4, finish, 0)
     whole(*ways[LAST], LAST).wait_send()
     whole(gsent, ggot, GRADS).wait_send()
     for g in range(FWD):
         whole(back.at[g], mine.at[g], GRADS + 1 + g).wait_send()
+
+
+def copy_out(*refs):
+    sources, results, sem = refs[:4], refs[4:8], refs[8]
+    copies = [pltpu.make_async_copy(a, b, sem.at[n]) for n, (a, b) in enumerate(zip(sources, results))]
+    for copy in copies:
+        copy.start()
+    for copy in copies:
+        copy.wait()
 
 
 ANY = pl.BlockSpec(memory_space=pltpu.HBM)
@@ -535,7 +555,7 @@
     operands = [state.transpose(0, 1, 3, 2, 4).reshape(6 * WZ, WY, NG), cotangent.transpose(0, 1, 3, 2, 4)]
     operands += [t[k] for k in ("tx", "tz", "tzk", "tzt", "tzkt", "perm", "back")]
     operands += [w_in.T, b_in[None, :], w_out]
-    grad, grad_in, grad_out, grad_bias = pl.pallas_call(
+    results = pl.pallas_call(
         main_kernel,
         out_shape=(sds((3, 2, WZ, WY, NG), F32), sds((8, FEAT), F32), sds((8, FEAT), F32), sds((1, 8), F32)),
         in_specs=[ANY] * 14,
@@ -576,6 +596,15 @@
             collective_id=0, has_side_effects=True, vmem_limit_bytes=LIMIT
         ),
     )(*[pltpu.with_memory_space_constraint(o, pltpu.HBM) for o in [*operands, t["ty"], t["tyk"]]])
+    free = pl.BlockSpec(memory_space=pl.ANY)
+    grad, grad_in, grad_out, grad_bias = pl.pallas_call(
+        copy_out,
+        out_shape=[sds(r.shape, r.dtype) for r in results],
+        in_specs=[free] * 4,
+        out_specs=[ANY] * 4,
+        scratch_shapes=[pltpu.SemaphoreType.DMA((4,))],
+        compiler_params=pltpu.CompilerParams(vmem_limit_bytes=8 * 1024 * 1024),
+    )(*results)
     return grad.transpose(0, 1, 3, 2, 4), grad_in, grad_out.T, grad_bias
 
 

time: 76.7 us -> 72.1 us (0.940)
  local copies, waits for them, and re-layouts: 2.92 us -> 0 us
  Pallas kernels: 73 us -> 71.4 us
    pallas_call x1, Pallas kernels: 73 us -> 70.1 us  [shards(): pl.pallas_call(main_kernel, out_shape=(sds((3, 2, WZ, WY, NG), F32), sds(...]
    unnamed x4 -> x0, local copies, waits for them, and re-layouts: 2.92 us -> none
    pallas_call x0 -> x1, Pallas kernels: none -> 1.25 us  [shards(): pl.pallas_call(copy_out, out_shape=[sds(r.shape, r.dtype) for r in result...]
where the time goes in v5:
time: 72.1 us; the launch traced here: 72 us
  Pallas kernels  71.4 us (99%)
    pallas_call x1, Pallas kernels, shards(): pl.pallas_call(main_kernel, out_shape=(sds((3, 2, WZ, WY, NG), F32), sds(...  70.1 us

profile of v5, /device:TPU:1, one launch (start us, length us, event | category | flops | bytes accessed | tf_op | source)
XLA Modules:
  0.0 72.0 jit_solution(3241103342756124091)
XLA Ops:
  0.6 70.1 %shard_map.165 = (f32[3,2,12,24,256]{4,3,2,1,0:T(8,128)S(1)}, f32[8,192]{1,0:T(8,128)S(1)}, f32[8,192]{1,0:T(8,128)S(1)}, f32[1,8]{1,0:T(1,128)S(1)}) custom-call(f32[72,24,256]{2,1,0:T(8,128)} %bitcast.8, f32[3,2,12,24,256]{4,3,2,1,0:T(8,128)} %bitcast.9, bf16[256,512]{1,0:T(8,128)(2,1)} %constant.18.clone.tx_hbm, bf16[256,192]{1,0:T(8,128)(2,1)} %constant.21.clone.tz_hbm, ...), custom_call_target="tpu_custom_call" | custom-call | tf_op jit(solution)/shard_map/pallas_call | solution.py:558
  70.7 1.3 %shard_map.166 = (f32[3,2,12,24,256]{4,3,2,1,0:T(8,128)}, f32[8,192]{1,0:T(8,128)}, f32[8,192]{1,0:T(8,128)}, f32[1,8]{1,0:T(1,128)}) custom-call(f32[3,2,12,24,256]{4,3,2,1,0:T(8,128)S(1)} %get-tuple-element.12.refs_0_, f32[8,192]{1,0:T(8,128)S(1)} %get-tuple-element.13.refs_1_, f32[8,192]{1,0:T(8,128)S(1)} %get-tuple-element.14.refs_2_, ...), custom_call_target="tpu_custom_call" | custom-call | tf_op jit(solution)/shard_map/pallas_call | solution.py:600

commit v6 on v5

--- a/solution.py
+++ b/solution.py
@@ -117,7 +117,7 @@
     out_ref, grad_in_ref, grad_out_ref, grad_bias_ref,
     state_ref, cot_ref, tx_ref, tz_ref, tzk_ref, tzt_ref, tzkt_ref, perm_ref, back_ref, w_in_t, b_row, w_out,
     s_ref, flat, sent, got, sent_few, got_few, v32, va32, o16, mine, gsent, ggot, ty_ref, tyk_ref,
-    win, wint, woutt, bias, gin, gout, hid_all, pre_all, feat_all, adj_all, ky_part, spare, load_sem, send_sem, recv_sem,
+    win, wint, woutt, bias, gin, gout, hid_all, pre_all, feat_all, adj_all, ky_part, load_sem, send_sem, recv_sem,
 ):
     j, l = lax.axis_index("px"), lax.axis_index("py")
     me = j * 8 + l
@@ -174,7 +174,7 @@
 
     ways = [(sent.at[g], got.at[g]) for g in range(3)] + [(sent_few, got_few)]
     for group in ORDER:
-        for load in [loads[0:2], loads[2:3], [], []][group]:
+        for load in {0: loads[0:2], 1: loads[2:3]}.get(group, []):
             load.wait()
         lanes = 128 if group == FEW else ROW
 
@@ -188,10 +188,13 @@
                 value = {}
                 if any(f >= 3 for f in fields):
                     scale = weight * retained
-                    v = [[scale * state_ref[(c * 2 + r) * WZ + m] for r in range(2)] for c in range(3)]
-                    value.update({3 + c: v[c] for c in range(3)})
-                    value[6] = [-(kz * v[0][1] - kx * v[2][1]), kz * v[0][0] - kx * v[2][0]]
-                    value[7] = [-(kx * v[1][1] - ky * v[0][1]), kx * v[1][0] - ky * v[0][0]]
+                    need = {c for f in fields for c in {6: (0, 2), 7: (0, 1)}.get(f, (f - 3,)) if f >= 3}
+                    v = {c: [scale * state_ref[(c * 2 + r) * WZ + m] for r in range(2)] for c in sorted(need)}
+                    value.update({3 + c: v[c] for c in v})
+                    if 6 in fields:
+                        value[6] = [-(kz * v[0][1] - kx * v[2][1]), kz * v[0][0] - kx * v[2][0]]
+                    if 7 in fields:
+                        value[7] = [-(kx * v[1][1] - ky * v[0][1]), kx * v[1][0] - ky * v[0][0]]
                 if any(f < 3 for f in fields):
                     inverse = 1.0 / jnp.maximum(square, 1.0)
                     scale = TIME_STEP * retained
@@ -229,7 +232,7 @@
             return carry
 
         lax.fori_loop(0, NDEV, pack, 0, unroll=4)
-        if group == 0:
+        if group == ORDER[0]:
             pl.semaphore_wait(barrier, NDEV - 1)
         send_all(*ways[group], group)
 
@@ -410,7 +413,7 @@
                 va32[h, pl.ds(bz, 48, stride=PITCH), :] = jnp.concatenate(lanes, axis=1)
         return carry
 
-    lax.fori_loop(0, 16, closure, 0, unroll=2)
+    lax.fori_loop(0, 16, closure, 0, unroll=4)
 
     whole(*ways[LAST], LAST).wait_recv()
     along_y(LAST)
@@ -438,7 +441,7 @@
     ninth = back_y(20, 0, ty_ref)
     for to in range(8):
         piece = ninth[:, to * SLOT : (to + 1) * SLOT]
-        spare[to] = jnp.concatenate([jnp.zeros((128, SPARE - 128), F32), piece], axis=1)
+        va32[0, to * 128 : (to + 1) * 128, :] = jnp.concatenate([jnp.zeros((128, SPARE - 128), F32), piece], axis=1)
 
     def products(k, carry):
         cols = pl.ds(pl.multiple_of(k * 1024, 1024), 1024)
@@ -451,7 +454,7 @@
 
     def slices(d, carry):
         rows = pl.ds(pl.multiple_of(d * 8, 8), 8)
-        extra = spare[d >> 3, pl.ds(pl.multiple_of((d & 7) * 16, 16), 16), :]
+        extra = va32[0, pl.ds(pl.multiple_of(d * 16, 16), 16), :]
         lo = jnp.concatenate([gin[rows, 0:128], FORCING * gout[rows, 0:128]], axis=0)
         hi = jnp.concatenate([gin[rows, 128:256], FORCING * gout[rows, 128:256]], axis=0)
         gsent[d, :, 0:128] = lo.astype(BF16)
@@ -480,7 +483,7 @@
                         o32[h, pl.ds(row, 128), :] = out[:, (2 * r + h) * 128 : (2 * r + h + 1) * 128]
             return carry
 
-        lax.fori_loop(0, 4, one, 0)
+        lax.fori_loop(0, 4, one, 0, unroll=4 if len(chunks) == 1 else 1)
 
     def finish(late):
         def one(mp, carry):
@@ -587,7 +590,6 @@
             pltpu.VMEM((256, 4096), BF16),
             pltpu.VMEM((FEAT, 4096), BF16),
             pltpu.VMEM((6, 128, ROW), F32),
-            pltpu.VMEM((8, 128, 128), F32),
             pltpu.SemaphoreType.DMA((16,)),
             pltpu.SemaphoreType.DMA((7,)),
             pltpu.SemaphoreType.DMA((7,)),

time: 72.1 us -> 70.7 us (0.981)
  Pallas kernels: 71.4 us -> 69.9 us
    pallas_call x1, Pallas kernels: 70.1 us -> 68.7 us  [shards(): pl.pallas_call(main_kernel, out_shape=(sds((3, 2, WZ, WY, NG), F32), sds(...]
where the time goes in v6:
time: 70.7 us; the launch traced here: 70.6 us
  Pallas kernels  69.9 us (99%)
    pallas_call x1, Pallas kernels, shards(): pl.pallas_call(main_kernel, out_shape=(sds((3, 2, WZ, WY, NG), F32), sds(...  68.7 us

profile of v6, /device:TPU:1, one launch (start us, length us, event | category | flops | bytes accessed | tf_op | source)
XLA Modules:
  0.0 70.6 jit_solution(8378385634539680704)
XLA Ops:
  0.6 68.7 %shard_map.165 = (f32[3,2,12,24,256]{4,3,2,1,0:T(8,128)S(1)}, f32[8,192]{1,0:T(8,128)S(1)}, f32[8,192]{1,0:T(8,128)S(1)}, f32[1,8]{1,0:T(1,128)S(1)}) custom-call(f32[72,24,256]{2,1,0:T(8,128)} %bitcast.8, f32[3,2,12,24,256]{4,3,2,1,0:T(8,128)} %bitcast.9, bf16[256,512]{1,0:T(8,128)(2,1)} %constant.18.clone.tx_hbm, bf16[256,192]{1,0:T(8,128)(2,1)} %constant.21.clone.tz_hbm, ...), custom_call_target="tpu_custom_call" | custom-call | tf_op jit(solution)/shard_map/pallas_call | solution.py:561
  69.3 1.3 %shard_map.166 = (f32[3,2,12,24,256]{4,3,2,1,0:T(8,128)}, f32[8,192]{1,0:T(8,128)}, f32[8,192]{1,0:T(8,128)}, f32[1,8]{1,0:T(1,128)}) custom-call(f32[3,2,12,24,256]{4,3,2,1,0:T(8,128)S(1)} %get-tuple-element.12.refs_0_, f32[8,192]{1,0:T(8,128)S(1)} %get-tuple-element.13.refs_1_, f32[8,192]{1,0:T(8,128)S(1)} %get-tuple-element.14.refs_2_, ...), custom_call_target="tpu_custom_call" | custom-call | tf_op jit(solution)/shard_map/pallas_call | solution.py:602

commit v7 on v6

--- a/solution.py
+++ b/solution.py
@@ -125,11 +125,11 @@
     l32, o32, kz_part, back = flat, v32, state_ref, sent
 
     def peer(k):
-        k = k + jnp.where(k >= 3, 1, 0)
-        dx = (k & 3) + 1
-        dy = dx + ((k >> 2) & 3)
-        px = (((x + dx) & 3) << 1) + ((core + (k >> 4)) & 1)
-        py = (((z + (k >> 5)) & 1) << 2) + ((y + dy) & 3)
+        k = k + jnp.where(k >= 6, 1, 0)
+        dx = ((k >> 1) & 3) + 1
+        dy = dx + ((k >> 3) & 3)
+        px = (((x + dx) & 3) << 1) + ((core + (k >> 5)) & 1)
+        py = (((z + k) & 1) << 2) + ((y + dy) & 3)
         return (px << 3) + py, {"px": px, "py": py}
 
     barrier = pltpu.get_barrier_semaphore()

time: 70.7 us -> 69.8 us (0.987)
  Pallas kernels: 69.9 us -> 69.1 us
    pallas_call x1, Pallas kernels: 68.7 us -> 67.8 us  [shards(): pl.pallas_call(main_kernel, out_shape=(sds((3, 2, WZ, WY, NG), F32), sds(...]
where the time goes in v7:
time: 69.8 us; the launch traced here: 69.7 us
  Pallas kernels  69.1 us (99%)
    pallas_call x1, Pallas kernels, shards(): pl.pallas_call(main_kernel, out_shape=(sds((3, 2, WZ, WY, NG), F32), sds(...  67.8 us

profile of v7, /device:TPU:1, one launch (start us, length us, event | category | flops | bytes accessed | tf_op | source)
XLA Modules:
  0.0 69.7 jit_solution(1127198627030041577)
XLA Ops:
  0.6 67.8 %shard_map.165 = (f32[3,2,12,24,256]{4,3,2,1,0:T(8,128)S(1)}, f32[8,192]{1,0:T(8,128)S(1)}, f32[8,192]{1,0:T(8,128)S(1)}, f32[1,8]{1,0:T(1,128)S(1)}) custom-call(f32[72,24,256]{2,1,0:T(8,128)} %bitcast.8, f32[3,2,12,24,256]{4,3,2,1,0:T(8,128)} %bitcast.9, bf16[256,512]{1,0:T(8,128)(2,1)} %constant.18.clone.tx_hbm, bf16[256,192]{1,0:T(8,128)(2,1)} %constant.21.clone.tz_hbm, ...), custom_call_target="tpu_custom_call" | custom-call | tf_op jit(solution)/shard_map/pallas_call | solution.py:561
  68.4 1.3 %shard_map.166 = (f32[3,2,12,24,256]{4,3,2,1,0:T(8,128)}, f32[8,192]{1,0:T(8,128)}, f32[8,192]{1,0:T(8,128)}, f32[1,8]{1,0:T(1,128)}) custom-call(f32[3,2,12,24,256]{4,3,2,1,0:T(8,128)S(1)} %get-tuple-element.12.refs_0_, f32[8,192]{1,0:T(8,128)S(1)} %get-tuple-element.13.refs_1_, f32[8,192]{1,0:T(8,128)S(1)} %get-tuple-element.14.refs_2_, ...), custom_call_target="tpu_custom_call" | custom-call | tf_op jit(solution)/shard_map/pallas_call | solution.py:602
